TPU v7x, 256 devices: a whole 4x4x8 slice. The times are simulated.
256 devices in a mesh: gx: 8 (over y, core), gy: 32 (over z, x).
Axes of the slice: x: 4, y: 4, z: 8, core: 2. Of those that a mesh axis runs over, the one named last changes fastest.
Arguments:
- tokens: bfloat16 [1024, 4096], P('gy', 'gx'), may hold values from -140 to 140
- cotangent: bfloat16 [1024, 4096], P('gy', 'gx'), may hold values from -6 to 6
- gate_weight: bfloat16 [4096, 14336], P('gx', 'gy'), may hold values from -5 to 5
- up_weight: bfloat16 [4096, 14336], P('gx', 'gy'), may hold values from -5 to 5
- down_weight: bfloat16 [14336, 4096], P('gy', 'gx'), may hold values from -5 to 5
Outputs:
- output: bfloat16 [1024, 4096], P('gy', 'gx')
- input_grad: bfloat16 [1024, 4096], P('gy', 'gx')
- gate_grad: bfloat16 [4096, 14336], P('gx', 'gy')
- up_grad: bfloat16 [4096, 14336], P('gx', 'gy')
- down_grad: bfloat16 [14336, 4096], P('gy', 'gx')
All inputs are finite; a program needn't handle non-finite values.
Results may differ from a plain program's by a relative error of at most 0.005.
The roundings to bfloat16 on the way count: a program that leaves them out, or rounds other values in their place, can miss the bound.
Values may be sent and summed in bfloat16 or wider, within the bound.
No kernel may reach another device: no remote copies, remote signals or barrier semaphores. Data moves between devices by JAX's collectives and lax.ppermute only.
A program may use at most 64 MiB of HBM per device.

v0:
```python
import jax
import jax.numpy as jnp
from jax import lax
from jax.experimental import pallas as pl
from jax.experimental.layout import Layout, with_layout_constraint
from jax.experimental.pallas import tpu as pltpu
from jax.sharding import Mesh
from jax.sharding import PartitionSpec as P


ROT_BLOCK = 128
HID_BLOCK = 64
NY, NC, NZ, NX = 4, 2, 8, 4
GX = ("y", "c")
GY = ("z", "x")
ALL = ("y", "c", "z", "x")


fp_top = 448.0
tiny = 1e-06
bf16 = jnp.bfloat16
f16 = jnp.float16
f32 = jnp.float32


def hadamard_table(block_size):
    row_ids = jnp.arange(block_size, dtype=jnp.int32)[:, None]
    col_ids = jnp.arange(block_size, dtype=jnp.int32)[None, :]
    shared = row_ids & col_ids
    parity = jnp.zeros((block_size, block_size), jnp.int32)
    for bit_pos in range(max(block_size.bit_length() - 1, 1)):
        parity = parity + (shared >> bit_pos & 1)
    return (1 - 2 * (parity % 2)).astype(f32)


def wide_table(block_size, i):
    parity = jnp.zeros((i.shape[0], i.shape[0]), jnp.int32)
    shared = i[:, None] & i[None, :]
    for bit_pos in range(block_size.bit_length() - 1):
        parity = parity + (shared >> bit_pos & 1)
    same = i[:, None] // block_size == i[None, :] // block_size
    return jnp.where(same, 1 - 2 * (parity % 2), 0).astype(bf16)


def rotate_cols(matrix, block_size, wide=None):
    row_total, col_total = matrix.shape
    table = hadamard_table(block_size)
    if wide is not None:
        turned = dot(matrix, wide, 1, 0)
    else:
        blocks = matrix.reshape(row_total, col_total // block_size, block_size)
        turned = jnp.einsum("rbk,kl->rbl", blocks, table, precision=lax.Precision.HIGHEST)
    return turned.reshape(row_total, col_total) * block_size ** (-0.5)


def rotate_rows(matrix, block_size, wide=None):
    row_total, col_total = matrix.shape
    table = hadamard_table(block_size)
    if wide is not None:
        turned = dot(wide, matrix, 1, 0)
    else:
        blocks = matrix.reshape(row_total // block_size, block_size, col_total)
        turned = jnp.einsum("kl,bkc->blc", table, blocks, precision=lax.Precision.HIGHEST)
    return turned.reshape(row_total, col_total) * block_size ** (-0.5)


def soft_cast(values, top):
    return (fp_top * jnp.tanh(values / (top + tiny))).astype(bf16)


def dot(left, right, left_dim, right_dim):
    return lax.dot_general(
        left, right, (((left_dim,), (right_dim,)), ((), ())), preferred_element_type=f32
    )


def after(values, *earlier):
    return lax.optimization_barrier((values, earlier))[0]


def swapped(value):
    return lax.ppermute(value, "c", [(0, 1), (1, 0)])


def shifted(value, axis, size, step):
    return lax.ppermute(value, axis, [(i, (i + step) % size) for i in range(size)])


def along_x(value, step, back=False):
    pairs = []
    for c in range(NC):
        for x in range(NX):
            to = c * NX + (x + (step if c == 0 else -step)) % NX
            pairs.append((to, c * NX + x) if back else (c * NX + x, to))
    return lax.ppermute(value, ("c", "x"), pairs)


def copied(value, axes, count):
    return lax.all_to_all(jnp.broadcast_to(value, (count, *value.shape)), axes, 0, 0, tiled=True)


def blocks_along_x(column):
    return column, shifted(column, "x", NX, 2), along_x(column, 1), along_x(column, 3)


def halves_along_x(blocks, first):
    column, far, near, last = blocks
    mine = jnp.concatenate([jnp.where(first, column, far), near], axis=0)
    other = jnp.concatenate([jnp.where(first, far, column), last], axis=0)
    return mine, other


def sum_along_x(mine, other, first, kind):
    rows, width = mine.shape[0] // 2, mine.shape[1]
    m, o = mine.reshape(2, rows, width), other.reshape(2, rows, width)
    sends = (
        m[1].astype(kind),
        o[1].astype(kind),
        jnp.where(first, o[0], m[0]).astype(kind),
    )
    near = along_x(sends[0], 1, back=True)
    last = along_x(sends[1], 3, back=True)
    far = shifted(sends[2], "x", NX, 2)
    column = jnp.where(first, m[0], o[0]) + near.astype(f32) + last.astype(f32) + far.astype(f32)
    return column.astype(kind), sends


def pieces_along_z(column):
    pieces = column.reshape(NZ, column.shape[0] // NZ, column.shape[1])
    return lax.all_to_all(pieces, "z", 0, 0, tiled=True)


def scatter_width(mine, theirs, kind):
    got = swapped(theirs.astype(kind))
    blocks = (mine + got.astype(f32)).reshape(NY, mine.shape[0] // NY, mine.shape[1])
    me = lax.axis_index("y")
    total = lax.dynamic_index_in_dim(blocks, me, 0, keepdims=False)
    sends = [
        lax.dynamic_index_in_dim(blocks, (me + step) % NY, 0, keepdims=False).astype(kind)
        for step in range(1, NY)
    ]
    for step in range(1, NY):
        total = total + shifted(sends[step - 1], "y", NY, step).astype(f32)
    return total


def join_kernel(me_ref, own_ref, got1_ref, got2_ref, got3_ref, out_ref):
    rows = own_ref.shape[0]
    for step, ref in enumerate((own_ref, got1_ref, got2_ref, got3_ref)):
        at = pl.multiple_of(((me_ref[0] + NY - step) & (NY - 1)) * rows, rows)
        out_ref[pl.ds(at, rows), :] = ref[...]


def gather_half(value):
    got = [shifted(value, "y", NY, step) for step in range(1, NY)]
    vmem = pl.BlockSpec(memory_space=pltpu.VMEM)
    mine = pl.pallas_call(
        join_kernel,
        out_shape=jax.ShapeDtypeStruct((NY * value.shape[0], value.shape[1]), value.dtype),
        in_specs=[pl.BlockSpec(memory_space=pltpu.SMEM)] + [vmem] * NY,
        out_specs=vmem,
        name="join",
    )(lax.axis_index("y")[None], value, *got)
    return mine, swapped(mine)


def middle_kernel(sums_ref, scales_ref, table_ref, out_ref, top_ref):
    wide = scales_ref.shape[1]
    table = table_ref[...]
    top = jnp.zeros((8, 128), f32)
    for at in range(0, wide, 128):
        gate = sums_ref[:, at : at + 128] * scales_ref[0:1, at : at + 128]
        up = sums_ref[:, wide + at : wide + at + 128] * scales_ref[1:2, at : at + 128]
        back = sums_ref[:, 2 * wide + at : 2 * wide + at + 128] * scales_ref[2:3, at : at + 128]
        sig = jax.nn.sigmoid(gate)
        hidden = (gate * sig * up).astype(bf16)
        turned = jnp.abs(jnp.dot(hidden, table, preferred_element_type=f32)) * HID_BLOCK**-0.5
        for row in range(0, turned.shape[0], 8):
            top = jnp.maximum(top, turned[row : row + 8])
        grad = jnp.zeros(back.shape, f32)
        for _ in range(3):
            term = back.astype(bf16)
            grad = grad + jnp.dot(term, table, preferred_element_type=f32)
            back = back - term.astype(f32)
        grad = grad * HID_BLOCK**-0.5
        gate_act = grad * up * sig * (1.0 + gate * (1.0 - sig))
        out_ref[:, at : at + 128] = gate_act.astype(bf16)
        out_ref[:, wide + at : wide + at + 128] = (grad * gate * sig).astype(bf16)
        out_ref[:, 2 * wide + at : 2 * wide + at + 128] = hidden
    top_ref[...] = top


def row_major(array):
    return with_layout_constraint(array, Layout(major_to_minor=tuple(range(array.ndim))))


def padded(array, dim):
    extra = -array.shape[dim] % 128
    widths = [(0, extra if d == dim else 0) for d in range(array.ndim)]
    return jnp.pad(array, widths)


def column_peaks(values):
    return jnp.max(jnp.abs(values), axis=0, keepdims=True)


def everyones(values):
    copies = jnp.broadcast_to(values, (NY * NC * NZ * NX, 1, values.shape[0]))
    return lax.all_to_all(copies, ALL, 0, 0, tiled=True).max(axis=(0, 1))


def rotate_rows_split(matrix, block_size, wide):
    total = 0.0
    for _ in range(3):
        term = lax.reduce_precision(matrix, 8, 7)
        total = total + dot(wide, term.astype(bf16), 1, 0)
        matrix = matrix - term
    return total * block_size ** (-0.5)


def layer(tokens, cotangent, gate_weight, up_weight, down_weight):
    hid = gate_weight.shape[1]
    rows, features = tokens.shape
    core = lax.axis_index("c")
    first = core == 0

    column = copied(jnp.concatenate([tokens, cotangent], axis=0), "z", NZ)
    token_column = column[:, :rows].reshape(NZ * rows, features)
    cot_column = column[:, rows:].reshape(NZ * rows, features)

    ids = lax.optimization_barrier(jnp.arange(features, dtype=jnp.int32))
    rot_wide, hid_wide = lax.optimization_barrier(
        (wide_table(ROT_BLOCK, ids), wide_table(HID_BLOCK, ids))
    )
    pair_rot = rotate_rows(
        jnp.concatenate([padded(gate_weight, 1), padded(up_weight, 1)], axis=1),
        ROT_BLOCK,
        rot_wide,
    )
    wide = pair_rot.shape[1] // 2
    down_rot = rotate_rows(padded(down_weight, 0), HID_BLOCK, hid_wide)
    token_rot = rotate_cols(tokens, ROT_BLOCK, rot_wide)
    tops = jnp.concatenate(
        [
            column_peaks(pair_rot[:, :wide]),
            column_peaks(pair_rot[:, wide:]),
            column_peaks(down_rot),
            column_peaks(token_rot),
        ],
        axis=0,
    )
    peaks = everyones(after(tops.max(axis=1), column))
    gate_peak, up_peak, down_peak, token_peak = peaks[0], peaks[1], peaks[2], peaks[3]
    pair_peak = jnp.where(jnp.arange(2 * wide) < wide, gate_peak, up_peak)[None, :]
    weight_pair = soft_cast(pair_rot, pair_peak)
    down_cast = soft_cast(down_rot, down_peak)

    mine_tokens, their_tokens = halves_along_x(blocks_along_x(token_column), first)
    mine_cot, their_cot = halves_along_x(blocks_along_x(cot_column), first)

    their_tok = soft_cast(rotate_cols(their_tokens, ROT_BLOCK, rot_wide), token_peak)
    mine_tok = soft_cast(rotate_cols(mine_tokens, ROT_BLOCK, rot_wide), token_peak)

    def part(tok, cot):
        return jnp.concatenate(
            [dot(tok, weight_pair, 1, 0) * 2.0**-12, dot(cot, down_cast, 1, 1) * 2.0**-6], axis=1
        )

    sums = scatter_width(part(mine_tok, mine_cot), part(their_tok, their_cot), f16)
    scales = jnp.stack(
        [
            token_peak * gate_peak / (fp_top * fp_top) * 2.0**12,
            token_peak * up_peak / (fp_top * fp_top) * 2.0**12,
            down_peak / fp_top * 2.0**6,
        ]
    )
    vmem = pl.BlockSpec(memory_space=pltpu.VMEM)
    acts, hidden_top = pl.pallas_call(
        middle_kernel,
        out_shape=(
            jax.ShapeDtypeStruct(sums.shape, bf16),
            jax.ShapeDtypeStruct((8, 128), f32),
        ),
        in_specs=[vmem] * 3,
        out_specs=(vmem, vmem),
        name="middle",
    )(sums, jnp.broadcast_to(scales[:, None], (3, wide)), hid_wide[:128, :128])
    mine_acts, their_acts = gather_half(acts)
    mine_act, their_act = mine_acts[:, : 2 * wide], their_acts[:, : 2 * wide]
    mine_hid, their_hid = mine_acts[:, 2 * wide :], their_acts[:, 2 * wide :]

    hidden_tops = copied(hidden_top.max(axis=0, keepdims=True), ALL, NY * NC * NZ * NX)

    def in_part(half):
        return dot(half[:, :wide], weight_pair[:, :wide], 1, 1) * (gate_peak / fp_top) + dot(
            half[:, wide:], weight_pair[:, wide:], 1, 1
        ) * (up_peak / fp_top)

    mine_in, their_in = in_part(mine_act), in_part(their_act)
    in_column, in_sends = sum_along_x(mine_in, their_in, first, bf16)

    hidden_peak = after(hidden_tops, in_sends).max()

    def out_part(half):
        cast = soft_cast(rotate_cols(half, HID_BLOCK, hid_wide), hidden_peak)
        return cast, dot(cast, down_cast, 1, 0) * 2.0**-13

    (mine_hid_cast, mine_out), (their_hid_cast, their_out) = (
        out_part(mine_hid),
        out_part(their_hid),
    )
    out_column, out_sends = sum_along_x(mine_out, their_out, first, f16)

    in_arrived = pieces_along_z(in_column)
    input_sum = in_arrived.astype(f32).sum(axis=0)
    input_grad = rotate_cols(input_sum, ROT_BLOCK).astype(bf16)
    out_arrived = pieces_along_z(after(out_column, in_arrived))
    out_sum = out_arrived.astype(f32).sum(axis=0)
    output = (out_sum * (hidden_peak * down_peak / (fp_top * fp_top) * 2.0**13)).astype(bf16)

    mine_hid_cast, their_hid_cast = after((mine_hid_cast, their_hid_cast), out_sends)
    down_dot = dot(mine_hid_cast, mine_cot, 0, 0) + dot(their_hid_cast, their_cot, 0, 0)
    down_grad = rotate_rows_split(down_dot * (hidden_peak / fp_top), HID_BLOCK, hid_wide)
    down_grad = down_grad[:hid].astype(bf16)
    mine_act, their_act = after((mine_act, their_act), in_column)
    pair_dot = dot(mine_tok, mine_act, 0, 0) + dot(their_tok, their_act, 0, 0)
    pair_grad = rotate_rows_split(pair_dot * (token_peak / fp_top), ROT_BLOCK, rot_wide)
    pair_grad = row_major(pair_grad.astype(bf16))
    return (
        output,
        input_grad,
        pair_grad[:, :hid],
        pair_grad[:, wide : wide + hid],
        down_grad,
    )


def solution(mesh):
    split = Mesh(mesh.devices.reshape(NY, NC, NZ, NX), ALL)
    placed = (P(GY, GX), P(GY, GX), P(GX, GY), P(GX, GY), P(GY, GX))
    return jax.shard_map(
        layer,
        mesh=split,
        in_specs=placed,
        out_specs=(P(GY, GX), P(GY, GX), P(GX, GY), P(GX, GY), P(GY, GX)),
        check_vma=False,
    )
```

profile of v0, /device:TPU:8, one launch (start us, length us, event | category | flops | bytes accessed | tf_op | source)
XLA Modules:
  0.0 222.6 jit_solution(9253644880898595110)
XLA Ops:
  2.4 8.5 %all-to-all-start = ((bf16[8,64,512]{2,1,0:T(8,128)(2,1)}), bf16[8,64,512]{2,1,0:T(8,128)(2,1)S(1)}, u32[]{:S(2)}, u32[]{:S(2)}) async-start(bf16[8,64,512]{2,1,0:T(8,128)(2,1)} %broadcast_in_dim.54), calls=%async_computation | async-start | bytes 1048576 | tf_op jit(solution)/shard_map/all_to_all | solution.py:99
  10.8 2.0 fusion.39
  16.8 11.5 %all-to-all-done = bf16[8,64,512]{2,1,0:T(8,128)(2,1)S(1)} async-done(((bf16[8,64,512]{2,1,0:T(8,128)(2,1)}), bf16[8,64,512]{2,1,0:T(8,128)(2,1)S(1)}, u32[]{:S(2)}, u32[]{:S(2)}) %all-to-all-start) | async-done | bytes 524320 | tf_op jit(solution)/shard_map/all_to_all | solution.py:99
  29.0 8.0 %all-to-all-start.1 = ((f32[256,1,4]{2,1,0:T(1,128)}), f32[256,1,4]{2,1,0:T(1,128)S(1)}, u32[]{:S(2)}, u32[]{:S(2)}) async-start(f32[256,1,4]{2,1,0:T(1,128)} %broadcast_in_dim.59), calls=%async_computation.1 | async-start | bytes 262144 | tf_op jit(solution)/shard_map/all_to_all | solution.py:209
  37.1 2.8 %collective-permute-start.5 = (bf16[256,512]{1,0:T(8,128)(2,1)S(1)}, bf16[256,512]{1,0:T(8,128)(2,1)}, u32[]{:S(2)}, u32[]{:S(2)}) collective-permute-start(bf16[256,512]{1,0:T(8,128)(2,1)S(1)} %bitcast.83), channel_id=1, source_target_pairs={{0,3},{1,0},{2,1},{3,2},{32,33},{33,34},{34,35},{35,32},{4,7},{5,4... | collective-permute-start | bytes 786440 | tf_op jit(solution)/shard_map/ppermute | solution.py:95
  43.6 5.4 %all-to-all-done.1 = f32[256,1,4]{2,1,0:T(1,128)S(1)} async-done(((f32[256,1,4]{2,1,0:T(1,128)}), f32[256,1,4]{2,1,0:T(1,128)S(1)}, u32[]{:S(2)}, u32[]{:S(2)}) %all-to-all-start.1) | async-done | bytes 4128 | tf_op jit(solution)/shard_map/all_to_all | solution.py:209
  51.2 1.9 multiply_convert_fusion.2
  65.3 2.1 collective-permute-start.6
  68.8 6.2 %collective-permute-done.3 = bf16[256,512]{1,0:T(8,128)(2,1)} collective-permute-done((bf16[256,512]{1,0:T(8,128)(2,1)S(1)}, bf16[256,512]{1,0:T(8,128)(2,1)}, u32[]{:S(2)}, u32[]{:S(2)}) %collective-permute-start.3) | collective-permute-done | bytes 262176 | tf_op jit(solution)/shard_map/ppermute | solution.py:95
  79.0 2.0 maximum_add_fusion
  85.7 2.2 collective-permute-start.8
  91.7 4.3 %collective-permute-done.7 = f16[128,1536]{1,0:T(8,128)(2,1)} collective-permute-done((f16[128,1536]{1,0:T(8,128)(2,1)}, f16[128,1536]{1,0:T(8,128)(2,1)}, u32[]{:S(2)}, u32[]{:S(2)}) %collective-permute-start.7) | collective-permute-done | bytes 393248 | tf_op jit(solution)/shard_map/ppermute | solution.py:86
  96.8 6.5 %collective-permute-done.8 = f16[128,1536]{1,0:T(8,128)(2,1)} collective-permute-done((f16[128,1536]{1,0:T(8,128)(2,1)S(1)}, f16[128,1536]{1,0:T(8,128)(2,1)}, u32[]{:S(2)}, u32[]{:S(2)}) %collective-permute-start.8) | collective-permute-done | bytes 393248 | tf_op jit(solution)/shard_map/ppermute | solution.py:86
  103.2 2.5 %fusion.67.sums_ref = f32[128,1536]{1,0:T(8,128)} fusion(f16[128,1536]{1,0:T(8,128)(2,1)} %collective-permute-done.9, f16[128,1536]{1,0:T(8,128)(2,1)} %collective-permute-done.8, f16[128,1536]{1,0:T(8,128)(2,1)} %collective-permute-done.7, f32[4,128,1536]{2,1,0:T(8,128)} %bitcast.79, s32[]{:T(128)S(6)} %select_n.125), kind=kLoop, calls=%fused_computation.118 | loop fusion | flops 1179648 | bytes 2752516 | tf_op jit(solution)/shard_map/add | solution.py:143
  106.4 2.3 %middle.1 = (bf16[128,1536]{1,0:T(8,128)(2,1)}, f32[8,128]{1,0:T(8,128)}) custom-call(f32[128,1536]{1,0:T(8,128)} %fusion.67.sums_ref, f32[3,512]{1,0:T(4,128)} %broadcast_in_dim.62.scales_ref, bf16[128,128]{1,0:T(8,128)(2,1)} %slice.121.table_ref), custom_call_target="tpu_custom_call" | custom-call | tf_op jit(solution)/shard_map/middle/pallas_call | solution.py:278
  110.7 2.5 %collective-permute-start.10 = (bf16[128,1536]{1,0:T(8,128)(2,1)}, bf16[128,1536]{1,0:T(8,128)(2,1)}, u32[]{:S(2)}, u32[]{:S(2)}) collective-permute-start(bf16[128,1536]{1,0:T(8,128)(2,1)} %get-tuple-element.19.own_ref), channel_id=1, source_target_pairs={{0,64},{64,128},{128,192},{192,0},{1,65},{65,129},{129,193},{193,1... | collective-permute-start | bytes 1179656 | tf_op jit(solution)/shard_map/ppermute | solution.py:86
  113.2 11.9 %collective-permute-done.12.got3_ref = bf16[128,1536]{1,0:T(8,128)(2,1)S(1)} collective-permute-done((bf16[128,1536]{1,0:T(8,128)(2,1)}, bf16[128,1536]{1,0:T(8,128)(2,1)S(1)}, u32[]{:S(2)}, u32[]{:S(2)}) %collective-permute-start.12) | collective-permute-done | bytes 393248 | tf_op jit(solution)/shard_map/ppermute | solution.py:86
  125.2 1.9 collective-permute-done.10.got1_ref
  127.1 2.6 %join.1 = bf16[512,1536]{1,0:T(8,128)(2,1)} custom-call(s32[1]{0:T(128)} %bitcast.me_ref, bf16[128,1536]{1,0:T(8,128)(2,1)} %get-tuple-element.19.own_ref, bf16[128,1536]{1,0:T(8,128)(2,1)} %collective-permute-done.10.got1_ref, bf16[128,1536]{1,0:T(8,128)(2,1)} %collective-permute-done.11.got2_ref, bf16[128,1536]{1,0:T(8,128)(2,1)} %copy-done.14), custom_call_target="tpu_custom_call" | custom-call | tf_op jit(solution)/shard_map/join/pallas_call | solution.py:157
  132.3 15.8 %all-to-all-start.2 = ((f32[256,1,128]{2,1,0:T(1,128)}), f32[256,1,128]{2,1,0:T(1,128)S(1)}, u32[]{:S(2)}, u32[]{:S(2)}) async-start(f32[256,1,128]{2,1,0:T(1,128)} %broadcast_in_dim.63), calls=%async_computation.2 | async-start | bytes 262144 | tf_op jit(solution)/shard_map/all_to_all | solution.py:99
  148.1 2.4 %slice.163 = bf16[512,1024]{1,0:T(8,128)(2,1)} slice(bf16[512,1536]{1,0:T(8,128)(2,1)} %join.1), slice={[0:512], [0:1024]} | slice | bytes 2097152 | tf_op jit(solution)/shard_map/slice | solution.py:289
  156.9 3.2 %all-to-all-done.2 = f32[256,1,128]{2,1,0:T(1,128)S(1)} async-done(((f32[256,1,128]{2,1,0:T(1,128)}), f32[256,1,128]{2,1,0:T(1,128)S(1)}, u32[]{:S(2)}, u32[]{:S(2)}) %all-to-all-start.2) | async-done | bytes 131104 | tf_op jit(solution)/shard_map/all_to_all | solution.py:99
  165.7 2.5 %collective-permute-start.17 = (bf16[256,512]{1,0:T(8,128)(2,1)}, bf16[256,512]{1,0:T(8,128)(2,1)}, u32[]{:S(2)}, u32[]{:S(2)}) collective-permute-start(bf16[256,512]{1,0:T(8,128)(2,1)} %get-tuple-element.59), channel_id=1, source_target_pairs={{1,0},{2,1},{3,2},{0,3},{35,32},{32,33},{33,34},{34,35},{5,4},{6,5... | collective-permute-start | bytes 786440 | tf_op jit(solution)/shard_map/ppermute | solution.py:95
  183.1 2.4 %slice.164 = bf16[512,1024]{1,0:T(8,128)(2,1)} slice(bf16[512,1536]{1,0:T(8,128)(2,1)} %collective-permute-done.13), slice={[0:512], [0:1024]} | slice | bytes 2097152 | tf_op jit(solution)/shard_map/slice | solution.py:289
  185.6 2.4 %fusion.65 = bf16[448,512]{1,0:T(8,128)(2,1)} fusion(f32[512,512]{1,0:T(8,128)S(1)} %copy-done.9, f32[512,512]{1,0:T(8,128)S(1)} %copy-done.10, f32[512,512]{1,0:T(8,128)} %fusion.70), kind=kLoop, calls=%fused_computation.114 | loop fusion | flops 917504 | bytes 3211264 | tf_op jit(solution)/shard_map/convert
  188.8 2.0 add_convert_fusion
  190.8 5.9 %all-to-all-start.3 = ((bf16[8,32,512]{2,1,0:T(8,128)(2,1)}), bf16[8,32,512]{2,1,0:T(8,128)(2,1)S(1)}, u32[]{:S(2)}, u32[]{:S(2)}) async-start(bf16[8,32,512]{2,1,0:T(8,128)(2,1)} %bitcast.19), calls=%async_computation.3 | async-start | bytes 524288 | tf_op jit(solution)/shard_map/all_to_all | solution.py:130
  196.7 2.2 fusion.134
  201.2 2.0 add_convert_fusion.1
  203.9 4.1 %all-to-all-done.3 = bf16[8,32,512]{2,1,0:T(8,128)(2,1)S(1)} async-done(((bf16[8,32,512]{2,1,0:T(8,128)(2,1)}), bf16[8,32,512]{2,1,0:T(8,128)(2,1)S(1)}, u32[]{:S(2)}, u32[]{:S(2)}) %all-to-all-start.3) | async-done | bytes 262176 | tf_op jit(solution)/shard_map/all_to_all | solution.py:130
  208.1 3.4 %all-to-all-start.4 = ((f16[8,32,512]{2,1,0:T(8,128)(2,1)}), f16[8,32,512]{2,1,0:T(8,128)(2,1)S(1)}, u32[]{:S(2)}, u32[]{:S(2)}) async-start(f16[8,32,512]{2,1,0:T(8,128)(2,1)} %bitcast.20), calls=%async_computation.4 | async-start | bytes 524288 | tf_op jit(solution)/shard_map/all_to_all | solution.py:130
  214.4 7.5 %all-to-all-done.4 = f16[8,32,512]{2,1,0:T(8,128)(2,1)S(1)} async-done(((f16[8,32,512]{2,1,0:T(8,128)(2,1)}), f16[8,32,512]{2,1,0:T(8,128)(2,1)S(1)}, u32[]{:S(2)}, u32[]{:S(2)}) %all-to-all-start.4) | async-done | bytes 262176 | tf_op jit(solution)/shard_map/all_to_all | solution.py:130
  (134 shorter events, 69.7 us)
Async XLA Ops:
  0.6 12.3 %copy-start.18 = (bf16[32,512]{1,0:T(8,128)(2,1)S(1)}, bf16[32,512]{1,0:T(8,128)(2,1)}, u32[]{:S(2)}) copy-start(bf16[32,512]{1,0:T(8,128)(2,1)} %param.5) | copy-start | bytes 98308
  0.6 12.5 %copy-start.20 = (bf16[512,448]{0,1:T(8,128)(2,1)S(1)}, bf16[512,448]{0,1:T(8,128)(2,1)}, u32[]{:S(2)}) copy-start(bf16[512,448]{0,1:T(8,128)(2,1)} %param.8) | copy-start | bytes 1376260
  0.7 12.5 %copy-start.21 = (bf16[512,448]{0,1:T(8,128)(2,1)S(1)}, bf16[512,448]{0,1:T(8,128)(2,1)}, u32[]{:S(2)}) copy-start(bf16[512,448]{0,1:T(8,128)(2,1)} %param.7) | copy-start | bytes 1376260
  2.4 26.0 %all-to-all-start = ((bf16[8,64,512]{2,1,0:T(8,128)(2,1)}), bf16[8,64,512]{2,1,0:T(8,128)(2,1)S(1)}, u32[]{:S(2)}, u32[]{:S(2)}) async-start(bf16[8,64,512]{2,1,0:T(8,128)(2,1)} %broadcast_in_dim.54), calls=%async_computation | async-start | bytes 1048576 | tf_op jit(solution)/shard_map/all_to_all | solution.py:99
  29.0 19.9 %all-to-all-start.1 = ((f32[256,1,4]{2,1,0:T(1,128)}), f32[256,1,4]{2,1,0:T(1,128)S(1)}, u32[]{:S(2)}, u32[]{:S(2)}) async-start(f32[256,1,4]{2,1,0:T(1,128)} %broadcast_in_dim.59), calls=%async_computation.1 | async-start | bytes 262144 | tf_op jit(solution)/shard_map/all_to_all | solution.py:209
  37.1 24.5 %collective-permute-start.5 = (bf16[256,512]{1,0:T(8,128)(2,1)S(1)}, bf16[256,512]{1,0:T(8,128)(2,1)}, u32[]{:S(2)}, u32[]{:S(2)}) collective-permute-start(bf16[256,512]{1,0:T(8,128)(2,1)S(1)} %bitcast.83), channel_id=1, source_target_pairs={{0,3},{1,0},{2,1},{3,2},{32,33},{33,34},{34,35},{35,32},{4,7},{5,4... | collective-permute-start | bytes 786440 | tf_op jit(solution)/shard_map/ppermute | solution.py:95
  39.8 20.7 %collective-permute-start.2 = (bf16[256,512]{1,0:T(8,128)(2,1)S(1)}, bf16[256,512]{1,0:T(8,128)(2,1)}, u32[]{:S(2)}, u32[]{:S(2)}) collective-permute-start(bf16[256,512]{1,0:T(8,128)(2,1)S(1)} %bitcast.84), channel_id=1, source_target_pairs={{0,2},{1,3},{2,0},{3,1},{4,6},{5,7},{6,4},{7,5},{8,10},{9,11},{10,... | collective-permute-start | bytes 786440 | tf_op jit(solution)/shard_map/ppermute | solution.py:86
  40.7 17.7 %collective-permute-start.4 = (bf16[256,512]{1,0:T(8,128)(2,1)S(1)}, bf16[256,512]{1,0:T(8,128)(2,1)}, u32[]{:S(2)}, u32[]{:S(2)}) collective-permute-start(bf16[256,512]{1,0:T(8,128)(2,1)S(1)} %bitcast.80), channel_id=1, source_target_pairs={{0,3},{1,0},{2,1},{3,2},{32,33},{33,34},{34,35},{35,32},{4,7},{5,4... | collective-permute-start | bytes 786440 | tf_op jit(solution)/shard_map/ppermute | solution.py:95
  41.9 14.8 %collective-permute-start = (bf16[256,512]{1,0:T(8,128)(2,1)S(1)}, bf16[256,512]{1,0:T(8,128)(2,1)S(1)}, u32[]{:S(2)}, u32[]{:S(2)}) collective-permute-start(bf16[256,512]{1,0:T(8,128)(2,1)S(1)} %bitcast.81), channel_id=1, source_target_pairs={{0,2},{1,3},{2,0},{3,1},{4,6},{5,7},{6,4},{7,5},{8,10},{9,11},{10,... | collective-permute-start | bytes 786440 | tf_op jit(solution)/shard_map/ppermute | solution.py:86
  55.1 116.0 %copy-start.3 = (bf16[512,512]{1,0:T(8,128)(2,1)}, bf16[512,512]{1,0:T(8,128)(2,1)S(1)}, u32[]{:S(2)}) copy-start(bf16[512,512]{1,0:T(8,128)(2,1)S(1)} %multiply_convert_fusion.3) | copy-start | bytes 1572868
  65.3 13.7 %collective-permute-start.6 = (f16[512,1536]{1,0:T(8,128)(2,1)}, f16[512,1536]{1,0:T(8,128)(2,1)}, u32[]{:S(2)}, u32[]{:S(2)}) collective-permute-start(f16[512,1536]{1,0:T(8,128)(2,1)} %pad_maximum_fusion), channel_id=1, source_target_pairs={{0,32},{32,0},{1,33},{33,1},{2,34},{34,2},{3,35},{35,3},{4,36},{36... | collective-permute-start | bytes 4718600 | tf_op jit(solution)/shard_map/ppermute | solution.py:82
  67.3 7.7 %collective-permute-start.3 = (bf16[256,512]{1,0:T(8,128)(2,1)S(1)}, bf16[256,512]{1,0:T(8,128)(2,1)}, u32[]{:S(2)}, u32[]{:S(2)}) collective-permute-start(bf16[256,512]{1,0:T(8,128)(2,1)S(1)} %bitcast.85), channel_id=1, source_target_pairs={{0,1},{1,2},{2,3},{3,0},{32,35},{33,32},{34,33},{35,34},{4,5},{5,6... | collective-permute-start | bytes 786440 | tf_op jit(solution)/shard_map/ppermute | solution.py:95
  68.5 9.2 %copy-start.17 = (bf16[256,512]{1,0:T(8,128)(2,1)S(1)}, bf16[256,512]{1,0:T(8,128)(2,1)}, u32[]{:S(2)}) copy-start(bf16[256,512]{1,0:T(8,128)(2,1)} %get-tuple-element.61) | copy-start | bytes 786436
  68.5 9.2 %collective-permute-start.1 = (bf16[256,512]{1,0:T(8,128)(2,1)S(1)}, bf16[256,512]{1,0:T(8,128)(2,1)S(1)}, u32[]{:S(2)}, u32[]{:S(2)}) collective-permute-start(bf16[256,512]{1,0:T(8,128)(2,1)S(1)} %bitcast.82), channel_id=1, source_target_pairs={{0,1},{1,2},{2,3},{3,0},{32,35},{33,32},{34,33},{35,34},{4,5},{5,6... | collective-permute-start | bytes 786440 | tf_op jit(solution)/shard_map/ppermute | solution.py:95
  83.6 12.3 %collective-permute-start.7 = (f16[128,1536]{1,0:T(8,128)(2,1)}, f16[128,1536]{1,0:T(8,128)(2,1)}, u32[]{:S(2)}, u32[]{:S(2)}) collective-permute-start(f16[128,1536]{1,0:T(8,128)(2,1)} %get-tuple-element.49), channel_id=1, source_target_pairs={{0,64},{64,128},{128,192},{192,0},{1,65},{65,129},{129,193},{193,1... | collective-permute-start | bytes 1179656 | tf_op jit(solution)/shard_map/ppermute | solution.py:86
  85.1 11.6 %collective-permute-start.9 = (f16[128,1536]{1,0:T(8,128)(2,1)}, f16[128,1536]{1,0:T(8,128)(2,1)}, u32[]{:S(2)}, u32[]{:S(2)}) collective-permute-start(f16[128,1536]{1,0:T(8,128)(2,1)} %get-tuple-element.50), channel_id=1, source_target_pairs={{0,192},{64,0},{128,64},{192,128},{1,193},{65,1},{129,65},{193,129... | collective-permute-start | bytes 1179656 | tf_op jit(solution)/shard_map/ppermute | solution.py:86
  85.7 17.6 %collective-permute-start.8 = (f16[128,1536]{1,0:T(8,128)(2,1)S(1)}, f16[128,1536]{1,0:T(8,128)(2,1)}, u32[]{:S(2)}, u32[]{:S(2)}) collective-permute-start(f16[128,1536]{1,0:T(8,128)(2,1)S(1)} %get-tuple-element.51), channel_id=1, source_target_pairs={{0,128},{64,192},{128,0},{192,64},{1,129},{65,193},{129,1},{193,65... | collective-permute-start | bytes 1179656 | tf_op jit(solution)/shard_map/ppermute | solution.py:86
  108.7 22.9 %copy-start.19 = (f32[8,128]{1,0:T(8,128)S(1)}, f32[8,128]{1,0:T(8,128)}, u32[]{:S(2)}) copy-start(f32[8,128]{1,0:T(8,128)} %get-tuple-element.20) | copy-start | bytes 12292
  108.7 16.5 %collective-permute-start.12 = (bf16[128,1536]{1,0:T(8,128)(2,1)}, bf16[128,1536]{1,0:T(8,128)(2,1)S(1)}, u32[]{:S(2)}, u32[]{:S(2)}) collective-permute-start(bf16[128,1536]{1,0:T(8,128)(2,1)} %get-tuple-element.19.own_ref), channel_id=1, source_target_pairs={{0,192},{64,0},{128,64},{192,128},{1,193},{65,1},{129,65},{193,129... | collective-permute-start | bytes 1179656 | tf_op jit(solution)/shard_map/ppermute | solution.py:86
  109.6 15.6 %collective-permute-start.11 = (bf16[128,1536]{1,0:T(8,128)(2,1)}, bf16[128,1536]{1,0:T(8,128)(2,1)}, u32[]{:S(2)}, u32[]{:S(2)}) collective-permute-start(bf16[128,1536]{1,0:T(8,128)(2,1)} %get-tuple-element.19.own_ref), channel_id=1, source_target_pairs={{0,128},{64,192},{128,0},{192,64},{1,129},{65,193},{129,1},{193,65... | collective-permute-start | bytes 1179656 | tf_op jit(solution)/shard_map/ppermute | solution.py:86
  110.7 16.4 %collective-permute-start.10 = (bf16[128,1536]{1,0:T(8,128)(2,1)}, bf16[128,1536]{1,0:T(8,128)(2,1)}, u32[]{:S(2)}, u32[]{:S(2)}) collective-permute-start(bf16[128,1536]{1,0:T(8,128)(2,1)} %get-tuple-element.19.own_ref), channel_id=1, source_target_pairs={{0,64},{64,128},{128,192},{192,0},{1,65},{65,129},{129,193},{193,1... | collective-permute-start | bytes 1179656 | tf_op jit(solution)/shard_map/ppermute | solution.py:86
  129.7 21.8 %collective-permute-start.13 = (bf16[512,1536]{1,0:T(8,128)(2,1)}, bf16[512,1536]{1,0:T(8,128)(2,1)}, u32[]{:S(2)}, u32[]{:S(2)}) collective-permute-start(bf16[512,1536]{1,0:T(8,128)(2,1)} %join.1), channel_id=1, source_target_pairs={{0,32},{32,0},{1,33},{33,1},{2,34},{34,2},{3,35},{35,3},{4,36},{36... | collective-permute-start | bytes 4718600 | tf_op jit(solution)/shard_map/ppermute | solution.py:82
  132.3 27.7 %all-to-all-start.2 = ((f32[256,1,128]{2,1,0:T(1,128)}), f32[256,1,128]{2,1,0:T(1,128)S(1)}, u32[]{:S(2)}, u32[]{:S(2)}) async-start(f32[256,1,128]{2,1,0:T(1,128)} %broadcast_in_dim.63), calls=%async_computation.2 | async-start | bytes 262144 | tf_op jit(solution)/shard_map/all_to_all | solution.py:99
  163.5 24.5 %collective-permute-start.19 = (bf16[256,512]{1,0:T(8,128)(2,1)}, bf16[256,512]{1,0:T(8,128)(2,1)}, u32[]{:S(2)}, u32[]{:S(2)}) collective-permute-start(bf16[256,512]{1,0:T(8,128)(2,1)} %get-tuple-element.57), channel_id=1, source_target_pairs={{0,2},{1,3},{2,0},{3,1},{4,6},{5,7},{6,4},{7,5},{8,10},{9,11},{10,... | collective-permute-start | bytes 786440 | tf_op jit(solution)/shard_map/ppermute | solution.py:86
  164.9 23.8 %collective-permute-start.18 = (bf16[256,512]{1,0:T(8,128)(2,1)}, bf16[256,512]{1,0:T(8,128)(2,1)}, u32[]{:S(2)}, u32[]{:S(2)}) collective-permute-start(bf16[256,512]{1,0:T(8,128)(2,1)} %get-tuple-element.58), channel_id=1, source_target_pairs={{3,0},{0,1},{1,2},{2,3},{33,32},{34,33},{35,34},{32,35},{7,4},{4,5... | collective-permute-start | bytes 786440 | tf_op jit(solution)/shard_map/ppermute | solution.py:95
  165.7 23.1 %collective-permute-start.17 = (bf16[256,512]{1,0:T(8,128)(2,1)}, bf16[256,512]{1,0:T(8,128)(2,1)}, u32[]{:S(2)}, u32[]{:S(2)}) collective-permute-start(bf16[256,512]{1,0:T(8,128)(2,1)} %get-tuple-element.59), channel_id=1, source_target_pairs={{1,0},{2,1},{3,2},{0,3},{35,32},{32,33},{33,34},{34,35},{5,4},{6,5... | collective-permute-start | bytes 786440 | tf_op jit(solution)/shard_map/ppermute | solution.py:95
  174.2 27.0 %collective-permute-start.14 = (f16[256,512]{1,0:T(8,128)(2,1)}, f16[256,512]{1,0:T(8,128)(2,1)}, u32[]{:S(2)}, u32[]{:S(2)}) collective-permute-start(f16[256,512]{1,0:T(8,128)(2,1)} %get-tuple-element.54), channel_id=1, source_target_pairs={{1,0},{2,1},{3,2},{0,3},{35,32},{32,33},{33,34},{34,35},{5,4},{6,5... | collective-permute-start | bytes 786440 | tf_op jit(solution)/shard_map/ppermute | solution.py:95
  174.6 26.6 %collective-permute-start.16 = (f16[256,512]{1,0:T(8,128)(2,1)}, f16[256,512]{1,0:T(8,128)(2,1)}, u32[]{:S(2)}, u32[]{:S(2)}) collective-permute-start(f16[256,512]{1,0:T(8,128)(2,1)} %get-tuple-element.55), channel_id=1, source_target_pairs={{0,2},{1,3},{2,0},{3,1},{4,6},{5,7},{6,4},{7,5},{8,10},{9,11},{10,... | collective-permute-start | bytes 786440 | tf_op jit(solution)/shard_map/ppermute | solution.py:86
  188.0 13.2 %collective-permute-start.15 = (f16[256,512]{1,0:T(8,128)(2,1)}, f16[256,512]{1,0:T(8,128)(2,1)}, u32[]{:S(2)}, u32[]{:S(2)}) collective-permute-start(f16[256,512]{1,0:T(8,128)(2,1)} %get-tuple-element.56), channel_id=1, source_target_pairs={{3,0},{0,1},{1,2},{2,3},{33,32},{34,33},{35,34},{32,35},{7,4},{4,5... | collective-permute-start | bytes 786440 | tf_op jit(solution)/shard_map/ppermute | solution.py:95
  190.8 8.1 %copy-start.12 = (bf16[512,512]{1,0:T(8,128)(2,1)S(1)}, bf16[512,512]{1,0:T(8,128)(2,1)}, u32[]{:S(2)}) copy-start(bf16[512,512]{1,0:T(8,128)(2,1)} %copy-done.11) | copy-start | bytes 1572868
  190.8 17.3 %all-to-all-start.3 = ((bf16[8,32,512]{2,1,0:T(8,128)(2,1)}), bf16[8,32,512]{2,1,0:T(8,128)(2,1)S(1)}, u32[]{:S(2)}, u32[]{:S(2)}) async-start(bf16[8,32,512]{2,1,0:T(8,128)(2,1)} %bitcast.19), calls=%async_computation.3 | async-start | bytes 524288 | tf_op jit(solution)/shard_map/all_to_all | solution.py:130
  208.1 13.9 %all-to-all-start.4 = ((f16[8,32,512]{2,1,0:T(8,128)(2,1)}), f16[8,32,512]{2,1,0:T(8,128)(2,1)S(1)}, u32[]{:S(2)}, u32[]{:S(2)}) async-start(f16[8,32,512]{2,1,0:T(8,128)(2,1)} %bitcast.20), calls=%async_computation.4 | async-start | bytes 524288 | tf_op jit(solution)/shard_map/all_to_all | solution.py:130
  (16 other events, 35.6 us)
where the time goes:
time: 225 us; the launch traced here: 223 us
  starting transfers between devices  67.4 us (30%)
  waiting for transfers between devices  66.6 us (30%)
  matrix products  30.5 us (14%)
  other arithmetic  27 us (12%)
  local copies, waits for them, and re-layouts  16.3 us (7%)
  between operations  10 us (4%)
  Pallas kernels  4.85 us (2%)
    dot_general x27, matrix products, dot(): lax.dot_general(left, right, (((left_dim,), (right_dim,)), ((), ())), pre...  30.2 us
    ppermute x10, waiting for transfers between devices, shifted(): lax.ppermute(value, axis, [(i, (i + step) % size) for i in range(size)])  26.3 us
    all_to_all x2, starting transfers between devices, copied(): lax.all_to_all(jnp.broadcast_to(value, (count, *value.shape)), axes, 0, 0...  24.2 us
    all_to_all x2, waiting for transfers between devices, copied(): lax.all_to_all(jnp.broadcast_to(value, (count, *value.shape)), axes, 0, 0...  14.7 us
    ppermute x10, starting transfers between devices, shifted(): lax.ppermute(value, axis, [(i, (i + step) % size) for i in range(size)])  14 us
    all_to_all x2, waiting for transfers between devices, pieces_along_z(): return lax.all_to_all(pieces, 'z', 0, 0, tiled=True)  11.7 us
    ppermute x8, starting transfers between devices, along_x(): return lax.ppermute(value, ('c', 'x'), pairs)  9.79 us
    all_to_all x2, starting transfers between devices, pieces_along_z(): return lax.all_to_all(pieces, 'z', 0, 0, tiled=True)  9.3 us
  transfers between devices with their start and end apart: 25, of which 14 were waited for; matrix products, arithmetic and copies ran while one was open for 25% of the time, Pallas kernels for 0%

commit v1 on v0

--- a/solution.py
+++ b/solution.py
@@ -2,7 +2,6 @@
 import jax.numpy as jnp
 from jax import lax
 from jax.experimental import pallas as pl
-from jax.experimental.layout import Layout, with_layout_constraint
 from jax.experimental.pallas import tpu as pltpu
 from jax.sharding import Mesh
 from jax.sharding import PartitionSpec as P
@@ -110,19 +109,12 @@
     return mine, other
 
 
-def sum_along_x(mine, other, first, kind):
-    rows, width = mine.shape[0] // 2, mine.shape[1]
-    m, o = mine.reshape(2, rows, width), other.reshape(2, rows, width)
-    sends = (
-        m[1].astype(kind),
-        o[1].astype(kind),
-        jnp.where(first, o[0], m[0]).astype(kind),
-    )
-    near = along_x(sends[0], 1, back=True)
-    last = along_x(sends[1], 3, back=True)
-    far = shifted(sends[2], "x", NX, 2)
-    column = jnp.where(first, m[0], o[0]) + near.astype(f32) + last.astype(f32) + far.astype(f32)
-    return column.astype(kind), sends
+def sum_along_x(keep, far, near, last):
+    near = along_x(near, 1, back=True)
+    last = along_x(last, 3, back=True)
+    far = shifted(far, "x", NX, 2)
+    total = keep + near.astype(f32) + last.astype(f32) + far.astype(f32)
+    return total.astype(bf16)
 
 
 def pieces_along_z(column):
@@ -190,8 +182,45 @@
     top_ref[...] = top
 
 
-def row_major(array):
-    return with_layout_constraint(array, Layout(major_to_minor=tuple(range(array.ndim))))
+def in_kernel(core_ref, scale_ref, mine_ref, their_ref, pair_ref, keep_ref, far_ref, near_ref, last_ref):
+    rows, wide = keep_ref.shape[0], pair_ref.shape[0] // 2
+    first = core_ref[0] == 0
+
+    def product(acts):
+        gate = dot(acts[:, :wide], pair_ref[:wide, :], 1, 0) * scale_ref[0]
+        return gate + dot(acts[:, wide:], pair_ref[wide:, :], 1, 0) * scale_ref[1]
+
+    near_ref[...] = product(mine_ref[rows:, : 2 * wide]).astype(bf16)
+    last_ref[...] = product(their_ref[rows:, : 2 * wide]).astype(bf16)
+    mine, their = mine_ref[:rows, : 2 * wide], their_ref[:rows, : 2 * wide]
+    far_ref[...] = product(jnp.where(first, their, mine)).astype(bf16)
+    keep_ref[...] = product(jnp.where(first, mine, their))
+
+
+def out_kernel(
+    core_ref, scale_ref, mine_ref, their_ref, table_ref, down_ref,
+    keep_ref, far_ref, near_ref, last_ref, mine_cast_ref, their_cast_ref,
+):
+    rows, wide = keep_ref.shape[0], down_ref.shape[0]
+    first = core_ref[0] == 0
+    table = table_ref[...]
+    for half_ref, cast_ref in ((mine_ref, mine_cast_ref), (their_ref, their_cast_ref)):
+        for at in range(0, wide, 128):
+            block = half_ref[:, 2 * wide + at : 2 * wide + at + 128]
+            turned = jnp.dot(block, table, preferred_element_type=f32) * scale_ref[0]
+            cast_ref[:, at : at + 128] = (fp_top * jnp.tanh(turned)).astype(bf16)
+    down = down_ref[...]
+    near_ref[...] = dot(mine_cast_ref[rows:, :], down, 1, 0).astype(bf16)
+    last_ref[...] = dot(their_cast_ref[rows:, :], down, 1, 0).astype(bf16)
+    mine, their = mine_cast_ref[:rows, :], their_cast_ref[:rows, :]
+    far_ref[...] = dot(jnp.where(first, their, mine), down, 1, 0).astype(bf16)
+    keep_ref[...] = dot(jnp.where(first, mine, their), down, 1, 0)
+
+
+def four_parts(rows, width):
+    return [jax.ShapeDtypeStruct((rows, width), f32)] + [
+        jax.ShapeDtypeStruct((rows, width), bf16)
+    ] * 3
 
 
 def padded(array, dim):
@@ -209,11 +238,12 @@
     return lax.all_to_all(copies, ALL, 0, 0, tiled=True).max(axis=(0, 1))
 
 
-def rotate_rows_split(matrix, block_size, wide):
+def rotate_split(matrix, block_size, wide, rows):
     total = 0.0
     for _ in range(3):
         term = lax.reduce_precision(matrix, 8, 7)
-        total = total + dot(wide, term.astype(bf16), 1, 0)
+        part = term.astype(bf16)
+        total = total + (dot(wide, part, 1, 0) if rows else dot(part, wide, 1, 0))
         matrix = matrix - term
     return total * block_size ** (-0.5)
 
@@ -232,18 +262,18 @@
     rot_wide, hid_wide = lax.optimization_barrier(
         (wide_table(ROT_BLOCK, ids), wide_table(HID_BLOCK, ids))
     )
-    pair_rot = rotate_rows(
-        jnp.concatenate([padded(gate_weight, 1), padded(up_weight, 1)], axis=1),
+    pair_rot = rotate_cols(
+        jnp.concatenate([padded(gate_weight.T, 0), padded(up_weight.T, 0)], axis=0),
         ROT_BLOCK,
         rot_wide,
     )
-    wide = pair_rot.shape[1] // 2
+    wide = pair_rot.shape[0] // 2
     down_rot = rotate_rows(padded(down_weight, 0), HID_BLOCK, hid_wide)
     token_rot = rotate_cols(tokens, ROT_BLOCK, rot_wide)
     tops = jnp.concatenate(
         [
-            column_peaks(pair_rot[:, :wide]),
-            column_peaks(pair_rot[:, wide:]),
+            column_peaks(pair_rot[:wide]),
+            column_peaks(pair_rot[wide:]),
             column_peaks(down_rot),
             column_peaks(token_rot),
         ],
@@ -251,22 +281,26 @@
     )
     peaks = everyones(after(tops.max(axis=1), column))
     gate_peak, up_peak, down_peak, token_peak = peaks[0], peaks[1], peaks[2], peaks[3]
-    pair_peak = jnp.where(jnp.arange(2 * wide) < wide, gate_peak, up_peak)[None, :]
+    pair_peak = jnp.where(jnp.arange(2 * wide) < wide, gate_peak, up_peak)[:, None]
     weight_pair = soft_cast(pair_rot, pair_peak)
     down_cast = soft_cast(down_rot, down_peak)
 
     mine_tokens, their_tokens = halves_along_x(blocks_along_x(token_column), first)
-    mine_cot, their_cot = halves_along_x(blocks_along_x(cot_column), first)
+    cot_blocks = blocks_along_x(cot_column)
 
     their_tok = soft_cast(rotate_cols(their_tokens, ROT_BLOCK, rot_wide), token_peak)
     mine_tok = soft_cast(rotate_cols(mine_tokens, ROT_BLOCK, rot_wide), token_peak)
 
-    def part(tok, cot):
-        return jnp.concatenate(
-            [dot(tok, weight_pair, 1, 0) * 2.0**-12, dot(cot, down_cast, 1, 1) * 2.0**-6], axis=1
-        )
-
-    sums = scatter_width(part(mine_tok, mine_cot), part(their_tok, their_cot), f16)
+    mine_pair = dot(mine_tok, weight_pair, 1, 1) * 2.0**-12
+    their_pair = (dot(their_tok, weight_pair, 1, 1) * 2.0**-12).astype(f16)
+    mine_cot, their_cot = halves_along_x(after(cot_blocks, mine_pair, their_pair), first)
+    their_back = (dot(their_cot, down_cast, 1, 1) * 2.0**-6).astype(f16)
+    mine_back = dot(mine_cot, down_cast, 1, 1) * 2.0**-6
+    sums = scatter_width(
+        jnp.concatenate([mine_pair, mine_back], axis=1),
+        jnp.concatenate([their_pair, their_back], axis=1),
+        f16,
+    )
     scales = jnp.stack(
         [
             token_peak * gate_peak / (fp_top * fp_top) * 2.0**12,
@@ -286,51 +320,60 @@
         name="middle",
     )(sums, jnp.broadcast_to(scales[:, None], (3, wide)), hid_wide[:128, :128])
     mine_acts, their_acts = gather_half(acts)
-    mine_act, their_act = mine_acts[:, : 2 * wide], their_acts[:, : 2 * wide]
-    mine_hid, their_hid = mine_acts[:, 2 * wide :], their_acts[:, 2 * wide :]
 
     hidden_tops = copied(hidden_top.max(axis=0, keepdims=True), ALL, NY * NC * NZ * NX)
 
-    def in_part(half):
-        return dot(half[:, :wide], weight_pair[:, :wide], 1, 1) * (gate_peak / fp_top) + dot(
-            half[:, wide:], weight_pair[:, wide:], 1, 1
-        ) * (up_peak / fp_top)
-
-    mine_in, their_in = in_part(mine_act), in_part(their_act)
-    in_column, in_sends = sum_along_x(mine_in, their_in, first, bf16)
-
-    hidden_peak = after(hidden_tops, in_sends).max()
-
-    def out_part(half):
-        cast = soft_cast(rotate_cols(half, HID_BLOCK, hid_wide), hidden_peak)
-        return cast, dot(cast, down_cast, 1, 0) * 2.0**-13
-
-    (mine_hid_cast, mine_out), (their_hid_cast, their_out) = (
-        out_part(mine_hid),
-        out_part(their_hid),
-    )
-    out_column, out_sends = sum_along_x(mine_out, their_out, first, f16)
+    smem = pl.BlockSpec(memory_space=pltpu.SMEM)
+    quarter = mine_acts.shape[0] // 2
+    in_parts = pl.pallas_call(
+        in_kernel,
+        out_shape=four_parts(quarter, features),
+        in_specs=[smem] * 2 + [vmem] * 3,
+        out_specs=[vmem] * 4,
+        name="in_part",
+    )(core[None], peaks[:2] / fp_top, mine_acts, their_acts, weight_pair)
+    in_column = sum_along_x(*in_parts)
+
+    hidden_peak = after(hidden_tops, *in_parts).max()
+    *out_parts, mine_hid_cast, their_hid_cast = pl.pallas_call(
+        out_kernel,
+        out_shape=four_parts(quarter, features)
+        + [jax.ShapeDtypeStruct((2 * quarter, wide), bf16)] * 2,
+        in_specs=[smem] * 2 + [vmem] * 4,
+        out_specs=[vmem] * 6,
+        name="out_part",
+    )(
+        core[None],
+        (HID_BLOCK**-0.5 / (hidden_peak + tiny))[None],
+        mine_acts,
+        their_acts,
+        hid_wide[:128, :128],
+        down_cast,
+    )
+    out_column = sum_along_x(*out_parts)
 
     in_arrived = pieces_along_z(in_column)
     input_sum = in_arrived.astype(f32).sum(axis=0)
     input_grad = rotate_cols(input_sum, ROT_BLOCK).astype(bf16)
     out_arrived = pieces_along_z(after(out_column, in_arrived))
     out_sum = out_arrived.astype(f32).sum(axis=0)
-    output = (out_sum * (hidden_peak * down_peak / (fp_top * fp_top) * 2.0**13)).astype(bf16)
-
-    mine_hid_cast, their_hid_cast = after((mine_hid_cast, their_hid_cast), out_sends)
+    output = (out_sum * (hidden_peak * down_peak / (fp_top * fp_top))).astype(bf16)
+
+    mine_hid_cast, their_hid_cast = after((mine_hid_cast, their_hid_cast), out_parts, in_column)
     down_dot = dot(mine_hid_cast, mine_cot, 0, 0) + dot(their_hid_cast, their_cot, 0, 0)
-    down_grad = rotate_rows_split(down_dot * (hidden_peak / fp_top), HID_BLOCK, hid_wide)
+    down_grad = rotate_split(down_dot * (hidden_peak / fp_top), HID_BLOCK, hid_wide, True)
     down_grad = down_grad[:hid].astype(bf16)
-    mine_act, their_act = after((mine_act, their_act), in_column)
-    pair_dot = dot(mine_tok, mine_act, 0, 0) + dot(their_tok, their_act, 0, 0)
-    pair_grad = rotate_rows_split(pair_dot * (token_peak / fp_top), ROT_BLOCK, rot_wide)
-    pair_grad = row_major(pair_grad.astype(bf16))
+    mine_tok, their_tok = after((mine_tok, their_tok), out_parts, in_column)
+    pair_dot = dot(mine_acts[:, : 2 * wide], mine_tok, 0, 0) + dot(
+        their_acts[:, : 2 * wide], their_tok, 0, 0
+    )
+    pair_grad = rotate_split(pair_dot * (token_peak / fp_top), ROT_BLOCK, rot_wide, False)
+    pair_grad = pair_grad.astype(bf16)
     return (
         output,
         input_grad,
-        pair_grad[:, :hid],
-        pair_grad[:, wide : wide + hid],
+        pair_grad[:hid].T,
+        pair_grad[wide : wide + hid].T,
         down_grad,
     )
 

time: 225 us -> 212 us (0.942)
  Pallas kernels: 4.85 us -> 13.1 us
  waiting for transfers between devices: 66.6 us -> 59.4 us
  matrix products: 30.5 us -> 24.2 us
    ppermute x8, waiting for transfers between devices: 8.53 us -> 0.26 us  [along_x(): return lax.ppermute(value, ('c', 'x'), pairs)]
    pallas_call x0 -> x2, Pallas kernels: none -> 8.25 us  [the longest x1 4.24 us: layer(): pl.pallas_call(in_kernel, out_shape=four_parts(quarter, features), in_spe...]
    dot_general x27 -> x19, matrix products: 30.2 us -> 24 us  [dot(): lax.dot_general(left, right, (((left_dim,), (right_dim,)), ((), ())), pre...]
    slice x3 -> x0, local copies, waits for them, and re-layouts: 4.89 us -> none  [the longest x2 4.82 us: layer(): mine_act, their_act = (mine_acts[:, :2 * wide], their_acts[:, :2 * wide])]
    all_to_all x2, starting transfers between devices: 24.2 us -> 19.5 us  [copied(): lax.all_to_all(jnp.broadcast_to(value, (count, *value.shape)), axes, 0, 0...]
    ppermute x10, waiting for transfers between devices: 26.3 us -> 30 us  [shifted(): lax.ppermute(value, axis, [(i, (i + step) % size) for i in range(size)])]
    ppermute x10, starting transfers between devices: 14 us -> 16.8 us  [shifted(): lax.ppermute(value, axis, [(i, (i + step) % size) for i in range(size)])]
    all_to_all x2, waiting for transfers between devices: 14.7 us -> 12.4 us  [copied(): lax.all_to_all(jnp.broadcast_to(value, (count, *value.shape)), axes, 0, 0...]
  transfers between devices with their start and end apart: 25 -> 25, of which waited for: 14 -> 13; matrix products, arithmetic and copies ran while one was open for 25% -> 21% of each run, Pallas kernels for 0% -> 4%
where the time goes in v1:
time: 212 us; the launch traced here: 211 us
  starting transfers between devices  66.2 us (31%)
  waiting for transfers between devices  59.4 us (28%)
  other arithmetic  25 us (12%)
  matrix products  24.2 us (11%)
  local copies, waits for them, and re-layouts  14.4 us (7%)
  Pallas kernels  13.1 us (6%)
  between operations  8.53 us (4%)
    ppermute x10, waiting for transfers between devices, shifted(): lax.ppermute(value, axis, [(i, (i + step) % size) for i in range(size)])  30 us
    dot_general x19, matrix products, dot(): lax.dot_general(left, right, (((left_dim,), (right_dim,)), ((), ())), pre...  24 us
    all_to_all x2, starting transfers between devices, copied(): lax.all_to_all(jnp.broadcast_to(value, (count, *value.shape)), axes, 0, 0...  19.5 us
    ppermute x10, starting transfers between devices, shifted(): lax.ppermute(value, axis, [(i, (i + step) % size) for i in range(size)])  16.8 us
    all_to_all x2, waiting for transfers between devices, copied(): lax.all_to_all(jnp.broadcast_to(value, (count, *value.shape)), axes, 0, 0...  12.4 us
    all_to_all x2, waiting for transfers between devices, pieces_along_z(): return lax.all_to_all(pieces, 'z', 0, 0, tiled=True)  10.9 us
    ppermute x8, starting transfers between devices, along_x(): return lax.ppermute(value, ('c', 'x'), pairs)  10.9 us
    all_to_all x2, starting transfers between devices, pieces_along_z(): return lax.all_to_all(pieces, 'z', 0, 0, tiled=True)  10.9 us
  transfers between devices with their start and end apart: 25, of which 13 were waited for; matrix products, arithmetic and copies ran while one was open for 21% of the time, Pallas kernels for 4%

profile of v1, /device:TPU:8, one launch (start us, length us, event | category | flops | bytes accessed | tf_op | source)
XLA Modules:
  0.0 210.8 jit_solution(13896852883099852822)
XLA Ops:
  2.4 8.5 %all-to-all-start = ((bf16[8,64,512]{2,1,0:T(8,128)(2,1)}), bf16[8,64,512]{2,1,0:T(8,128)(2,1)S(1)}, u32[]{:S(2)}, u32[]{:S(2)}) async-start(bf16[8,64,512]{2,1,0:T(8,128)(2,1)} %broadcast_in_dim.61), calls=%async_computation | async-start | bytes 1048576 | tf_op jit(solution)/shard_map/all_to_all | solution.py:98
  16.8 11.5 %all-to-all-done = bf16[8,64,512]{2,1,0:T(8,128)(2,1)S(1)} async-done(((bf16[8,64,512]{2,1,0:T(8,128)(2,1)}), bf16[8,64,512]{2,1,0:T(8,128)(2,1)S(1)}, u32[]{:S(2)}, u32[]{:S(2)}) %all-to-all-start) | async-done | bytes 524320 | tf_op jit(solution)/shard_map/all_to_all | solution.py:98
  29.0 8.0 %all-to-all-start.1 = ((f32[256,1,4]{2,1,0:T(1,128)}), f32[256,1,4]{2,1,0:T(1,128)S(1)}, u32[]{:S(2)}, u32[]{:S(2)}) async-start(f32[256,1,4]{2,1,0:T(1,128)} %broadcast_in_dim.66), calls=%async_computation.1 | async-start | bytes 262144 | tf_op jit(solution)/shard_map/all_to_all | solution.py:238
  37.1 3.1 %collective-permute-start = (bf16[256,512]{1,0:T(8,128)(2,1)S(1)}, bf16[256,512]{1,0:T(8,128)(2,1)}, u32[]{:S(2)}, u32[]{:S(2)}) collective-permute-start(bf16[256,512]{1,0:T(8,128)(2,1)S(1)} %bitcast.82), channel_id=1, source_target_pairs={{0,2},{1,3},{2,0},{3,1},{4,6},{5,7},{6,4},{7,5},{8,10},{9,11},{10,... | collective-permute-start | bytes 786440 | tf_op jit(solution)/shard_map/ppermute | solution.py:85
  42.8 2.6 %collective-permute-start.3 = (bf16[256,512]{1,0:T(8,128)(2,1)S(1)}, bf16[256,512]{1,0:T(8,128)(2,1)}, u32[]{:S(2)}, u32[]{:S(2)}) collective-permute-start(bf16[256,512]{1,0:T(8,128)(2,1)S(1)} %bitcast.79), channel_id=1, source_target_pairs={{0,1},{1,2},{2,3},{3,0},{32,35},{33,32},{34,33},{35,34},{4,5},{5,6... | collective-permute-start | bytes 786440 | tf_op jit(solution)/shard_map/ppermute | solution.py:94
  45.4 3.7 %all-to-all-done.1 = f32[256,1,4]{2,1,0:T(1,128)S(1)} async-done(((f32[256,1,4]{2,1,0:T(1,128)}), f32[256,1,4]{2,1,0:T(1,128)S(1)}, u32[]{:S(2)}, u32[]{:S(2)}) %all-to-all-start.1) | async-done | bytes 4128 | tf_op jit(solution)/shard_map/all_to_all | solution.py:238
  60.5 2.1 convolution_multiply_fusion
  71.0 2.1 collective-permute-done.6
  77.9 2.4 %collective-permute-start.8 = (f16[128,1536]{1,0:T(8,128)(2,1)S(1)}, f16[128,1536]{1,0:T(8,128)(2,1)S(1)}, u32[]{:S(2)}, u32[]{:S(2)}) collective-permute-start(f16[128,1536]{1,0:T(8,128)(2,1)S(1)} %get-tuple-element.59), channel_id=1, source_target_pairs={{0,128},{64,192},{128,0},{192,64},{1,129},{65,193},{129,1},{193,65... | collective-permute-start | bytes 1179656 | tf_op jit(solution)/shard_map/ppermute | solution.py:85
  85.0 3.9 %collective-permute-done.7 = f16[128,1536]{1,0:T(8,128)(2,1)S(1)} collective-permute-done((f16[128,1536]{1,0:T(8,128)(2,1)S(1)}, f16[128,1536]{1,0:T(8,128)(2,1)S(1)}, u32[]{:S(2)}, u32[]{:S(2)}) %collective-permute-start.7) | collective-permute-done | bytes 393248 | tf_op jit(solution)/shard_map/ppermute | solution.py:85
  88.8 2.6 %collective-permute-done.8 = f16[128,1536]{1,0:T(8,128)(2,1)S(1)} collective-permute-done((f16[128,1536]{1,0:T(8,128)(2,1)S(1)}, f16[128,1536]{1,0:T(8,128)(2,1)S(1)}, u32[]{:S(2)}, u32[]{:S(2)}) %collective-permute-start.8) | collective-permute-done | bytes 393248 | tf_op jit(solution)/shard_map/ppermute | solution.py:85
  91.4 7.4 %collective-permute-done.9 = f16[128,1536]{1,0:T(8,128)(2,1)} collective-permute-done((f16[128,1536]{1,0:T(8,128)(2,1)S(1)}, f16[128,1536]{1,0:T(8,128)(2,1)}, u32[]{:S(2)}, u32[]{:S(2)}) %collective-permute-start.9) | collective-permute-done | bytes 393248 | tf_op jit(solution)/shard_map/ppermute | solution.py:85
  98.8 2.3 %fusion.60.sums_ref = f32[128,1536]{1,0:T(8,128)} fusion(f16[128,1536]{1,0:T(8,128)(2,1)} %collective-permute-done.9, f16[128,1536]{1,0:T(8,128)(2,1)S(1)} %collective-permute-done.8, f16[128,1536]{1,0:T(8,128)(2,1)S(1)} %collective-permute-done.7, f32[4,128,1536]{2,1,0:T(8,128)} %bitcast.77, s32[]{:T(128)S(6)} %select_n.107), kind=kLoop, calls=%fused_computation.103 | loop fusion | flops 1179648 | bytes 2752516 | tf_op jit(solution)/shard_map/add | solution.py:135
  101.8 2.3 %middle.1 = (bf16[128,1536]{1,0:T(8,128)(2,1)}, f32[8,128]{1,0:T(8,128)}) custom-call(f32[128,1536]{1,0:T(8,128)} %fusion.60.sums_ref, f32[3,512]{1,0:T(4,128)} %broadcast_in_dim.69.scales_ref, bf16[128,128]{1,0:T(8,128)(2,1)} %slice.55.table_ref), custom_call_target="tpu_custom_call" | custom-call | tf_op jit(solution)/shard_map/middle/pallas_call | solution.py:312
  104.6 2.4 %collective-permute-start.11 = (bf16[128,1536]{1,0:T(8,128)(2,1)}, bf16[128,1536]{1,0:T(8,128)(2,1)S(1)}, u32[]{:S(2)}, u32[]{:S(2)}) collective-permute-start(bf16[128,1536]{1,0:T(8,128)(2,1)} %get-tuple-element.38.own_ref), channel_id=1, source_target_pairs={{0,128},{64,192},{128,0},{192,64},{1,129},{65,193},{129,1},{193,65... | collective-permute-start | bytes 1179656 | tf_op jit(solution)/shard_map/ppermute | solution.py:85
  109.1 7.1 %collective-permute-done.10.got1_ref = bf16[128,1536]{1,0:T(8,128)(2,1)S(1)} collective-permute-done((bf16[128,1536]{1,0:T(8,128)(2,1)}, bf16[128,1536]{1,0:T(8,128)(2,1)S(1)}, u32[]{:S(2)}, u32[]{:S(2)}) %collective-permute-start.10) | collective-permute-done | bytes 393248 | tf_op jit(solution)/shard_map/ppermute | solution.py:85
  116.2 2.2 %collective-permute-done.11.got2_ref = bf16[128,1536]{1,0:T(8,128)(2,1)S(1)} collective-permute-done((bf16[128,1536]{1,0:T(8,128)(2,1)}, bf16[128,1536]{1,0:T(8,128)(2,1)S(1)}, u32[]{:S(2)}, u32[]{:S(2)}) %collective-permute-start.11) | collective-permute-done | bytes 393248 | tf_op jit(solution)/shard_map/ppermute | solution.py:85
  118.4 6.9 %collective-permute-done.12.got3_ref = bf16[128,1536]{1,0:T(8,128)(2,1)S(1)} collective-permute-done((bf16[128,1536]{1,0:T(8,128)(2,1)}, bf16[128,1536]{1,0:T(8,128)(2,1)S(1)}, u32[]{:S(2)}, u32[]{:S(2)}) %collective-permute-start.12) | collective-permute-done | bytes 393248 | tf_op jit(solution)/shard_map/ppermute | solution.py:85
  126.0 2.6 %join.1.mine_ref = bf16[512,1536]{1,0:T(8,128)(2,1)} custom-call(s32[1]{0:T(128)} %bitcast.21.me_ref, bf16[128,1536]{1,0:T(8,128)(2,1)} %get-tuple-element.38.own_ref, bf16[128,1536]{1,0:T(8,128)(2,1)} %copy-done.18, bf16[128,1536]{1,0:T(8,128)(2,1)} %copy-done.19, bf16[128,1536]{1,0:T(8,128)(2,1)} %copy-done.20), custom_call_target="tpu_custom_call" | custom-call | tf_op jit(solution)/shard_map/join/pallas_call | solution.py:149
  129.9 11.0 %all-to-all-start.2 = ((f32[256,1,128]{2,1,0:T(1,128)}), f32[256,1,128]{2,1,0:T(1,128)S(1)}, u32[]{:S(2)}, u32[]{:S(2)}) async-start(f32[256,1,128]{2,1,0:T(1,128)} %broadcast_in_dim.70), calls=%async_computation.2 | async-start | bytes 262144 | tf_op jit(solution)/shard_map/all_to_all | solution.py:98
  142.2 4.2 %in_part.1 = (f32[256,512]{1,0:T(8,128)}, bf16[256,512]{1,0:T(8,128)(2,1)}, bf16[256,512]{1,0:T(8,128)(2,1)}, bf16[256,512]{1,0:T(8,128)(2,1)}) custom-call(s32[1]{0:T(128)} %bitcast.core_ref, f32[2]{0:T(128)} %slice_multiply_fusion.scale_ref, bf16[512,1536]{1,0:T(8,128)(2,1)} %join.1.mine_ref, bf16[512,1536]{1,0:T(8,128)(2,1)} %copy-done.2, ...), custom_call_target="tpu_custom_call" | custom-call | tf_op jit(solution)/shard_map/in_part/pallas_call | solution.py:328
  146.4 2.7 %collective-permute-start.17 = (bf16[256,512]{1,0:T(8,128)(2,1)}, bf16[256,512]{1,0:T(8,128)(2,1)S(1)}, u32[]{:S(2)}, u32[]{:S(2)}) collective-permute-start(bf16[256,512]{1,0:T(8,128)(2,1)} %get-tuple-element.41), channel_id=1, source_target_pairs={{1,0},{2,1},{3,2},{0,3},{35,32},{32,33},{33,34},{34,35},{5,4},{6,5... | collective-permute-start | bytes 786440 | tf_op jit(solution)/shard_map/ppermute | solution.py:94
  149.1 2.3 %collective-permute-start.19 = (bf16[256,512]{1,0:T(8,128)(2,1)}, bf16[256,512]{1,0:T(8,128)(2,1)S(1)}, u32[]{:S(2)}, u32[]{:S(2)}) collective-permute-start(bf16[256,512]{1,0:T(8,128)(2,1)} %get-tuple-element.40), channel_id=1, source_target_pairs={{0,2},{1,3},{2,0},{3,1},{4,6},{5,7},{6,4},{7,5},{8,10},{9,11},{10,... | collective-permute-start | bytes 786440 | tf_op jit(solution)/shard_map/ppermute | solution.py:85
  156.3 4.0 %out_part.1 = (f32[256,512]{1,0:T(8,128)}, bf16[256,512]{1,0:T(8,128)(2,1)}, bf16[256,512]{1,0:T(8,128)(2,1)}, bf16[256,512]{1,0:T(8,128)(2,1)}, bf16[512,512]{1,0:T(8,128)(2,1)}, /*index=5*/bf16[512,512]{1,0:T(8,128)(2,1)}) custom-call(s32[1]{0:T(128)} %bitcast.core_ref, f32[1]{0:T(128)} %bitcast.22.scale_ref, bf16[512,1536]{1,0:T(8,128)(2,1)} %join.1.mine_ref, ...), custom_call_target="tpu_custom_call" | custom-call | tf_op jit(solution)/shard_map/out_part/pallas_call | solution.py:338
  176.2 2.1 fusion.34
  178.3 7.3 %all-to-all-start.3 = ((bf16[8,32,512]{2,1,0:T(8,128)(2,1)}), bf16[8,32,512]{2,1,0:T(8,128)(2,1)S(1)}, u32[]{:S(2)}, u32[]{:S(2)}) async-start(bf16[8,32,512]{2,1,0:T(8,128)(2,1)} %bitcast.23), calls=%async_computation.3 | async-start | bytes 524288 | tf_op jit(solution)/shard_map/all_to_all | solution.py:122
  185.6 3.0 %fusion.58 = bf16[448,512]{1,0:T(8,128)(2,1)} fusion(f32[512,512]{1,0:T(8,128)} %fusion.61, f32[512,512]{1,0:T(8,128)} %fusion.64, f32[512,512]{1,0:T(8,128)} %fusion.63), kind=kLoop, calls=%fused_computation.99 | loop fusion | flops 917504 | bytes 3211264 | tf_op jit(solution)/shard_map/convert
  188.6 2.1 add_convert_fusion.1
  192.5 3.5 %all-to-all-done.3 = bf16[8,32,512]{2,1,0:T(8,128)(2,1)S(1)} async-done(((bf16[8,32,512]{2,1,0:T(8,128)(2,1)}), bf16[8,32,512]{2,1,0:T(8,128)(2,1)S(1)}, u32[]{:S(2)}, u32[]{:S(2)}) %all-to-all-start.3) | async-done | bytes 262176 | tf_op jit(solution)/shard_map/all_to_all | solution.py:122
  196.0 3.6 %all-to-all-start.4 = ((bf16[8,32,512]{2,1,0:T(8,128)(2,1)}), bf16[8,32,512]{2,1,0:T(8,128)(2,1)S(1)}, u32[]{:S(2)}, u32[]{:S(2)}) async-start(bf16[8,32,512]{2,1,0:T(8,128)(2,1)} %bitcast.24), calls=%async_computation.4 | async-start | bytes 524288 | tf_op jit(solution)/shard_map/all_to_all | solution.py:122
  199.7 2.1 %slice_bitcast_fusion = (bf16[512,448]{0,1:T(8,128)(2,1)}, bf16[512,448]{0,1:T(8,128)(2,1)}) fusion(bf16[1024,512]{1,0:T(8,128)(2,1)} %multiply_convert_fusion), kind=kLoop, calls=%fused_computation.124 | loop fusion | bytes 1835008 | tf_op jit(solution)/shard_map/transpose | solution.py:376
  202.8 7.4 %all-to-all-done.4 = bf16[8,32,512]{2,1,0:T(8,128)(2,1)S(1)} async-done(((bf16[8,32,512]{2,1,0:T(8,128)(2,1)}), bf16[8,32,512]{2,1,0:T(8,128)(2,1)S(1)}, u32[]{:S(2)}, u32[]{:S(2)}) %all-to-all-start.4) | async-done | bytes 262176 | tf_op jit(solution)/shard_map/all_to_all | solution.py:122
  (137 shorter events, 63.3 us)
Async XLA Ops:
  0.6 12.3 %copy-start.25 = (bf16[32,512]{1,0:T(8,128)(2,1)S(1)}, bf16[32,512]{1,0:T(8,128)(2,1)}, u32[]{:S(2)}) copy-start(bf16[32,512]{1,0:T(8,128)(2,1)} %param.5) | copy-start | bytes 98308
  0.6 12.5 %copy-start.28 = (bf16[512,448]{0,1:T(8,128)(2,1)S(1)}, bf16[512,448]{0,1:T(8,128)(2,1)}, u32[]{:S(2)}) copy-start(bf16[512,448]{0,1:T(8,128)(2,1)} %param.7) | copy-start | bytes 1376260
  0.7 12.5 %copy-start.27 = (bf16[512,448]{0,1:T(8,128)(2,1)S(1)}, bf16[512,448]{0,1:T(8,128)(2,1)}, u32[]{:S(2)}) copy-start(bf16[512,448]{0,1:T(8,128)(2,1)} %param.8) | copy-start | bytes 1376260
  2.4 26.0 %all-to-all-start = ((bf16[8,64,512]{2,1,0:T(8,128)(2,1)}), bf16[8,64,512]{2,1,0:T(8,128)(2,1)S(1)}, u32[]{:S(2)}, u32[]{:S(2)}) async-start(bf16[8,64,512]{2,1,0:T(8,128)(2,1)} %broadcast_in_dim.61), calls=%async_computation | async-start | bytes 1048576 | tf_op jit(solution)/shard_map/all_to_all | solution.py:98
  12.9 68.3 %copy-start.5 = (bf16[512,512]{1,0:T(8,128)(2,1)}, bf16[512,512]{1,0:T(8,128)(2,1)S(1)}, u32[]{:S(2)}) copy-start(bf16[512,512]{1,0:T(8,128)(2,1)S(1)} %get-tuple-element.31) | copy-start | bytes 1572868
  29.0 20.0 %all-to-all-start.1 = ((f32[256,1,4]{2,1,0:T(1,128)}), f32[256,1,4]{2,1,0:T(1,128)S(1)}, u32[]{:S(2)}, u32[]{:S(2)}) async-start(f32[256,1,4]{2,1,0:T(1,128)} %broadcast_in_dim.66), calls=%async_computation.1 | async-start | bytes 262144 | tf_op jit(solution)/shard_map/all_to_all | solution.py:238
  37.1 18.8 %collective-permute-start = (bf16[256,512]{1,0:T(8,128)(2,1)S(1)}, bf16[256,512]{1,0:T(8,128)(2,1)}, u32[]{:S(2)}, u32[]{:S(2)}) collective-permute-start(bf16[256,512]{1,0:T(8,128)(2,1)S(1)} %bitcast.82), channel_id=1, source_target_pairs={{0,2},{1,3},{2,0},{3,1},{4,6},{5,7},{6,4},{7,5},{8,10},{9,11},{10,... | collective-permute-start | bytes 786440 | tf_op jit(solution)/shard_map/ppermute | solution.py:85
  40.1 22.4 %collective-permute-start.5 = (bf16[256,512]{1,0:T(8,128)(2,1)S(1)}, bf16[256,512]{1,0:T(8,128)(2,1)}, u32[]{:S(2)}, u32[]{:S(2)}) collective-permute-start(bf16[256,512]{1,0:T(8,128)(2,1)S(1)} %bitcast.83), channel_id=1, source_target_pairs={{0,3},{1,0},{2,1},{3,2},{32,33},{33,34},{34,35},{35,32},{4,7},{5,4... | collective-permute-start | bytes 786440 | tf_op jit(solution)/shard_map/ppermute | solution.py:94
  41.3 16.9 %collective-permute-start.1 = (bf16[256,512]{1,0:T(8,128)(2,1)S(1)}, bf16[256,512]{1,0:T(8,128)(2,1)}, u32[]{:S(2)}, u32[]{:S(2)}) collective-permute-start(bf16[256,512]{1,0:T(8,128)(2,1)S(1)} %bitcast.84), channel_id=1, source_target_pairs={{0,1},{1,2},{2,3},{3,0},{32,35},{33,32},{34,33},{35,34},{4,5},{5,6... | collective-permute-start | bytes 786440 | tf_op jit(solution)/shard_map/ppermute | solution.py:94
  42.2 22.6 %collective-permute-start.2 = (bf16[256,512]{1,0:T(8,128)(2,1)S(1)}, bf16[256,512]{1,0:T(8,128)(2,1)S(1)}, u32[]{:S(2)}, u32[]{:S(2)}) collective-permute-start(bf16[256,512]{1,0:T(8,128)(2,1)S(1)} %bitcast.78), channel_id=1, source_target_pairs={{0,2},{1,3},{2,0},{3,1},{4,6},{5,7},{6,4},{7,5},{8,10},{9,11},{10,... | collective-permute-start | bytes 786440 | tf_op jit(solution)/shard_map/ppermute | solution.py:85
  42.8 22.2 %collective-permute-start.3 = (bf16[256,512]{1,0:T(8,128)(2,1)S(1)}, bf16[256,512]{1,0:T(8,128)(2,1)}, u32[]{:S(2)}, u32[]{:S(2)}) collective-permute-start(bf16[256,512]{1,0:T(8,128)(2,1)S(1)} %bitcast.79), channel_id=1, source_target_pairs={{0,1},{1,2},{2,3},{3,0},{32,35},{33,32},{34,33},{35,34},{4,5},{5,6... | collective-permute-start | bytes 786440 | tf_op jit(solution)/shard_map/ppermute | solution.py:94
  55.3 12.0 %copy-start.13 = (bf16[512,512]{1,0:T(8,128)(2,1)}, bf16[512,512]{1,0:T(8,128)(2,1)S(1)}, u32[]{:S(2)}) copy-start(bf16[512,512]{1,0:T(8,128)(2,1)S(1)} %multiply_convert_fusion.3.down_ref) | copy-start | bytes 1572868
  55.9 9.6 %collective-permute-start.4 = (bf16[256,512]{1,0:T(8,128)(2,1)S(1)}, bf16[256,512]{1,0:T(8,128)(2,1)S(1)}, u32[]{:S(2)}, u32[]{:S(2)}) collective-permute-start(bf16[256,512]{1,0:T(8,128)(2,1)S(1)} %bitcast.80), channel_id=1, source_target_pairs={{0,3},{1,0},{2,1},{3,2},{32,33},{33,34},{34,35},{35,32},{4,7},{5,4... | collective-permute-start | bytes 786440 | tf_op jit(solution)/shard_map/ppermute | solution.py:94
  69.3 3.8 %collective-permute-start.6 = (f16[512,1536]{1,0:T(8,128)(2,1)}, f16[512,1536]{1,0:T(8,128)(2,1)}, u32[]{:S(2)}, u32[]{:S(2)}) collective-permute-start(f16[512,1536]{1,0:T(8,128)(2,1)} %pad_maximum_fusion), channel_id=1, source_target_pairs={{0,32},{32,0},{1,33},{33,1},{2,34},{34,2},{3,35},{35,3},{4,36},{36... | collective-permute-start | bytes 4718600 | tf_op jit(solution)/shard_map/ppermute | solution.py:81
  76.8 12.1 %collective-permute-start.7 = (f16[128,1536]{1,0:T(8,128)(2,1)S(1)}, f16[128,1536]{1,0:T(8,128)(2,1)S(1)}, u32[]{:S(2)}, u32[]{:S(2)}) collective-permute-start(f16[128,1536]{1,0:T(8,128)(2,1)S(1)} %get-tuple-element.57), channel_id=1, source_target_pairs={{0,64},{64,128},{128,192},{192,0},{1,65},{65,129},{129,193},{193,1... | collective-permute-start | bytes 1179656 | tf_op jit(solution)/shard_map/ppermute | solution.py:85
  77.9 13.5 %collective-permute-start.8 = (f16[128,1536]{1,0:T(8,128)(2,1)S(1)}, f16[128,1536]{1,0:T(8,128)(2,1)S(1)}, u32[]{:S(2)}, u32[]{:S(2)}) collective-permute-start(f16[128,1536]{1,0:T(8,128)(2,1)S(1)} %get-tuple-element.59), channel_id=1, source_target_pairs={{0,128},{64,192},{128,0},{192,64},{1,129},{65,193},{129,1},{193,65... | collective-permute-start | bytes 1179656 | tf_op jit(solution)/shard_map/ppermute | solution.py:85
  80.3 18.5 %collective-permute-start.9 = (f16[128,1536]{1,0:T(8,128)(2,1)S(1)}, f16[128,1536]{1,0:T(8,128)(2,1)}, u32[]{:S(2)}, u32[]{:S(2)}) collective-permute-start(f16[128,1536]{1,0:T(8,128)(2,1)S(1)} %get-tuple-element.58), channel_id=1, source_target_pairs={{0,192},{64,0},{128,64},{192,128},{1,193},{65,1},{129,65},{193,129... | collective-permute-start | bytes 1179656 | tf_op jit(solution)/shard_map/ppermute | solution.py:85
  104.0 25.2 %copy-start.26 = (f32[8,128]{1,0:T(8,128)S(1)}, f32[8,128]{1,0:T(8,128)}, u32[]{:S(2)}) copy-start(f32[8,128]{1,0:T(8,128)} %get-tuple-element.37) | copy-start | bytes 12292
  104.0 12.2 %collective-permute-start.10 = (bf16[128,1536]{1,0:T(8,128)(2,1)}, bf16[128,1536]{1,0:T(8,128)(2,1)S(1)}, u32[]{:S(2)}, u32[]{:S(2)}) collective-permute-start(bf16[128,1536]{1,0:T(8,128)(2,1)} %get-tuple-element.38.own_ref), channel_id=1, source_target_pairs={{0,64},{64,128},{128,192},{192,0},{1,65},{65,129},{129,193},{193,1... | collective-permute-start | bytes 1179656 | tf_op jit(solution)/shard_map/ppermute | solution.py:85
  104.6 13.7 %collective-permute-start.11 = (bf16[128,1536]{1,0:T(8,128)(2,1)}, bf16[128,1536]{1,0:T(8,128)(2,1)S(1)}, u32[]{:S(2)}, u32[]{:S(2)}) collective-permute-start(bf16[128,1536]{1,0:T(8,128)(2,1)} %get-tuple-element.38.own_ref), channel_id=1, source_target_pairs={{0,128},{64,192},{128,0},{192,64},{1,129},{65,193},{129,1},{193,65... | collective-permute-start | bytes 1179656 | tf_op jit(solution)/shard_map/ppermute | solution.py:85
  107.0 18.2 %collective-permute-start.12 = (bf16[128,1536]{1,0:T(8,128)(2,1)}, bf16[128,1536]{1,0:T(8,128)(2,1)S(1)}, u32[]{:S(2)}, u32[]{:S(2)}) collective-permute-start(bf16[128,1536]{1,0:T(8,128)(2,1)} %get-tuple-element.38.own_ref), channel_id=1, source_target_pairs={{0,192},{64,0},{128,64},{192,128},{1,193},{65,1},{129,65},{193,129... | collective-permute-start | bytes 1179656 | tf_op jit(solution)/shard_map/ppermute | solution.py:85
  128.7 12.3 %collective-permute-start.13 = (bf16[512,1536]{1,0:T(8,128)(2,1)}, bf16[512,1536]{1,0:T(8,128)(2,1)S(1)}, u32[]{:S(2)}, u32[]{:S(2)}) collective-permute-start(bf16[512,1536]{1,0:T(8,128)(2,1)} %join.1.mine_ref), channel_id=1, source_target_pairs={{0,32},{32,0},{1,33},{33,1},{2,34},{34,2},{3,35},{35,3},{4,36},{36... | collective-permute-start | bytes 4718600 | tf_op jit(solution)/shard_map/ppermute | solution.py:81
  129.9 23.0 %all-to-all-start.2 = ((f32[256,1,128]{2,1,0:T(1,128)}), f32[256,1,128]{2,1,0:T(1,128)S(1)}, u32[]{:S(2)}, u32[]{:S(2)}) async-start(f32[256,1,128]{2,1,0:T(1,128)} %broadcast_in_dim.70), calls=%async_computation.2 | async-start | bytes 262144 | tf_op jit(solution)/shard_map/all_to_all | solution.py:98
  146.4 17.6 %copy-start.16 = (f32[256,512]{1,0:T(8,128)S(1)}, f32[256,512]{1,0:T(8,128)}, u32[]{:S(2)}) copy-start(f32[256,512]{1,0:T(8,128)} %get-tuple-element.39) | copy-start | bytes 1572868
  146.4 16.3 %collective-permute-start.17 = (bf16[256,512]{1,0:T(8,128)(2,1)}, bf16[256,512]{1,0:T(8,128)(2,1)S(1)}, u32[]{:S(2)}, u32[]{:S(2)}) collective-permute-start(bf16[256,512]{1,0:T(8,128)(2,1)} %get-tuple-element.41), channel_id=1, source_target_pairs={{1,0},{2,1},{3,2},{0,3},{35,32},{32,33},{33,34},{34,35},{5,4},{6,5... | collective-permute-start | bytes 786440 | tf_op jit(solution)/shard_map/ppermute | solution.py:94
  149.1 15.0 %collective-permute-start.18 = (bf16[256,512]{1,0:T(8,128)(2,1)}, bf16[256,512]{1,0:T(8,128)(2,1)S(1)}, u32[]{:S(2)}, u32[]{:S(2)}) collective-permute-start(bf16[256,512]{1,0:T(8,128)(2,1)} %get-tuple-element.42), channel_id=1, source_target_pairs={{3,0},{0,1},{1,2},{2,3},{33,32},{34,33},{35,34},{32,35},{7,4},{4,5... | collective-permute-start | bytes 786440 | tf_op jit(solution)/shard_map/ppermute | solution.py:94
  149.1 15.0 %collective-permute-start.19 = (bf16[256,512]{1,0:T(8,128)(2,1)}, bf16[256,512]{1,0:T(8,128)(2,1)S(1)}, u32[]{:S(2)}, u32[]{:S(2)}) collective-permute-start(bf16[256,512]{1,0:T(8,128)(2,1)} %get-tuple-element.40), channel_id=1, source_target_pairs={{0,2},{1,3},{2,0},{3,1},{4,6},{5,7},{6,4},{7,5},{8,10},{9,11},{10,... | collective-permute-start | bytes 786440 | tf_op jit(solution)/shard_map/ppermute | solution.py:85
  160.4 28.2 %collective-permute-start.14 = (bf16[256,512]{1,0:T(8,128)(2,1)}, bf16[256,512]{1,0:T(8,128)(2,1)}, u32[]{:S(2)}, u32[]{:S(2)}) collective-permute-start(bf16[256,512]{1,0:T(8,128)(2,1)} %get-tuple-element.45), channel_id=1, source_target_pairs={{1,0},{2,1},{3,2},{0,3},{35,32},{32,33},{33,34},{34,35},{5,4},{6,5... | collective-permute-start | bytes 786440 | tf_op jit(solution)/shard_map/ppermute | solution.py:94
  161.9 26.6 %collective-permute-start.15 = (bf16[256,512]{1,0:T(8,128)(2,1)}, bf16[256,512]{1,0:T(8,128)(2,1)}, u32[]{:S(2)}, u32[]{:S(2)}) collective-permute-start(bf16[256,512]{1,0:T(8,128)(2,1)} %get-tuple-element.46), channel_id=1, source_target_pairs={{3,0},{0,1},{1,2},{2,3},{33,32},{34,33},{35,34},{32,35},{7,4},{4,5... | collective-permute-start | bytes 786440 | tf_op jit(solution)/shard_map/ppermute | solution.py:94
  162.7 25.9 %collective-permute-start.16 = (bf16[256,512]{1,0:T(8,128)(2,1)}, bf16[256,512]{1,0:T(8,128)(2,1)}, u32[]{:S(2)}, u32[]{:S(2)}) collective-permute-start(bf16[256,512]{1,0:T(8,128)(2,1)} %get-tuple-element.47), channel_id=1, source_target_pairs={{0,2},{1,3},{2,0},{3,1},{4,6},{5,7},{6,4},{7,5},{8,10},{9,11},{10,... | collective-permute-start | bytes 786440 | tf_op jit(solution)/shard_map/ppermute | solution.py:85
  178.3 17.8 %all-to-all-start.3 = ((bf16[8,32,512]{2,1,0:T(8,128)(2,1)}), bf16[8,32,512]{2,1,0:T(8,128)(2,1)S(1)}, u32[]{:S(2)}, u32[]{:S(2)}) async-start(bf16[8,32,512]{2,1,0:T(8,128)(2,1)} %bitcast.23), calls=%async_computation.3 | async-start | bytes 524288 | tf_op jit(solution)/shard_map/all_to_all | solution.py:122
  196.0 14.1 %all-to-all-start.4 = ((bf16[8,32,512]{2,1,0:T(8,128)(2,1)}), bf16[8,32,512]{2,1,0:T(8,128)(2,1)S(1)}, u32[]{:S(2)}, u32[]{:S(2)}) async-start(bf16[8,32,512]{2,1,0:T(8,128)(2,1)} %bitcast.24), calls=%async_computation.4 | async-start | bytes 524288 | tf_op jit(solution)/shard_map/all_to_all | solution.py:122
  (23 other events, 87.3 us)

commit v2 on v1

--- a/solution.py
+++ b/solution.py
@@ -122,15 +122,22 @@
     return lax.all_to_all(pieces, "z", 0, 0, tiled=True)
 
 
-def scatter_width(mine, theirs, kind):
-    got = swapped(theirs.astype(kind))
-    blocks = (mine + got.astype(f32)).reshape(NY, mine.shape[0] // NY, mine.shape[1])
+def sum_with_other_core(mine, theirs):
+    total = mine + swapped(theirs).astype(f32)
+    return total.reshape(NY, mine.shape[0] // NY, mine.shape[1])
+
+
+def scatter_width(blocks, kind):
     me = lax.axis_index("y")
-    total = lax.dynamic_index_in_dim(blocks, me, 0, keepdims=False)
-    sends = [
-        lax.dynamic_index_in_dim(blocks, (me + step) % NY, 0, keepdims=False).astype(kind)
-        for step in range(1, NY)
-    ]
+
+    def block(step):
+        picked = [
+            lax.dynamic_index_in_dim(b, (me + step) % NY, 0, keepdims=False) for b in blocks
+        ]
+        return jnp.concatenate(picked, axis=1)
+
+    sends = [block(step).astype(kind) for step in range(1, NY)]
+    total = block(0)
     for step in range(1, NY):
         total = total + shifted(sends[step - 1], "y", NY, step).astype(f32)
     return total
@@ -145,14 +152,10 @@
 
 def gather_half(value):
     got = [shifted(value, "y", NY, step) for step in range(1, NY)]
-    vmem = pl.BlockSpec(memory_space=pltpu.VMEM)
-    mine = pl.pallas_call(
-        join_kernel,
-        out_shape=jax.ShapeDtypeStruct((NY * value.shape[0], value.shape[1]), value.dtype),
-        in_specs=[pl.BlockSpec(memory_space=pltpu.SMEM)] + [vmem] * NY,
-        out_specs=vmem,
-        name="join",
-    )(lax.axis_index("y")[None], value, *got)
+    shape = (NY * value.shape[0], value.shape[1])
+    (mine,) = call(
+        join_kernel, [(shape, value.dtype)], [lax.axis_index("y")[None]], [value, *got], None
+    )
     return mine, swapped(mine)
 
 
@@ -182,45 +185,72 @@
     top_ref[...] = top
 
 
-def in_kernel(core_ref, scale_ref, mine_ref, their_ref, pair_ref, keep_ref, far_ref, near_ref, last_ref):
-    rows, wide = keep_ref.shape[0], pair_ref.shape[0] // 2
-    first = core_ref[0] == 0
-
-    def product(acts):
-        gate = dot(acts[:, :wide], pair_ref[:wide, :], 1, 0) * scale_ref[0]
-        return gate + dot(acts[:, wide:], pair_ref[wide:, :], 1, 0) * scale_ref[1]
-
-    near_ref[...] = product(mine_ref[rows:, : 2 * wide]).astype(bf16)
-    last_ref[...] = product(their_ref[rows:, : 2 * wide]).astype(bf16)
-    mine, their = mine_ref[:rows, : 2 * wide], their_ref[:rows, : 2 * wide]
-    far_ref[...] = product(jnp.where(first, their, mine)).astype(bf16)
-    keep_ref[...] = product(jnp.where(first, mine, their))
-
-
-def out_kernel(
-    core_ref, scale_ref, mine_ref, their_ref, table_ref, down_ref,
-    keep_ref, far_ref, near_ref, last_ref, mine_cast_ref, their_cast_ref,
+def in_product(acts, pair_ref, scale_ref):
+    wide = pair_ref.shape[0] // 2
+    gate = dot(acts[:, :wide], pair_ref[:wide, :], 1, 0) * scale_ref[0]
+    return gate + dot(acts[:, wide:], pair_ref[wide:, :], 1, 0) * scale_ref[1]
+
+
+def place_parts(first, mine, their, keep_ref, far_ref):
+    far_ref[...] = jnp.where(first, their, mine).astype(bf16)
+    keep_ref[...] = jnp.where(first, mine, their)
+
+
+def in_mine_kernel(scale_ref, acts_ref, pair_ref, part_ref, near_ref):
+    rows, both = part_ref.shape[0], pair_ref.shape[0]
+    near_ref[...] = in_product(acts_ref[rows:, :both], pair_ref, scale_ref).astype(bf16)
+    part_ref[...] = in_product(acts_ref[:rows, :both], pair_ref, scale_ref)
+
+
+def in_their_kernel(
+    core_ref, scale_ref, acts_ref, pair_ref, part_ref, keep_ref, far_ref, last_ref
 ):
-    rows, wide = keep_ref.shape[0], down_ref.shape[0]
-    first = core_ref[0] == 0
-    table = table_ref[...]
-    for half_ref, cast_ref in ((mine_ref, mine_cast_ref), (their_ref, their_cast_ref)):
-        for at in range(0, wide, 128):
-            block = half_ref[:, 2 * wide + at : 2 * wide + at + 128]
-            turned = jnp.dot(block, table, preferred_element_type=f32) * scale_ref[0]
-            cast_ref[:, at : at + 128] = (fp_top * jnp.tanh(turned)).astype(bf16)
-    down = down_ref[...]
-    near_ref[...] = dot(mine_cast_ref[rows:, :], down, 1, 0).astype(bf16)
-    last_ref[...] = dot(their_cast_ref[rows:, :], down, 1, 0).astype(bf16)
-    mine, their = mine_cast_ref[:rows, :], their_cast_ref[:rows, :]
-    far_ref[...] = dot(jnp.where(first, their, mine), down, 1, 0).astype(bf16)
-    keep_ref[...] = dot(jnp.where(first, mine, their), down, 1, 0)
-
-
-def four_parts(rows, width):
-    return [jax.ShapeDtypeStruct((rows, width), f32)] + [
-        jax.ShapeDtypeStruct((rows, width), bf16)
-    ] * 3
+    rows, both = part_ref.shape[0], pair_ref.shape[0]
+    last_ref[...] = in_product(acts_ref[rows:, :both], pair_ref, scale_ref).astype(bf16)
+    their = in_product(acts_ref[:rows, :both], pair_ref, scale_ref)
+    place_parts(core_ref[0] == 0, part_ref[...], their, keep_ref, far_ref)
+
+
+def cast_hidden(tops_ref, acts_ref, table_ref, cast_ref):
+    table, wide = table_ref[...], cast_ref.shape[1]
+    top = jnp.max(jnp.max(tops_ref[...], axis=0, keepdims=True))
+    scale = HID_BLOCK**-0.5 / jnp.full((1, 128), top + tiny, f32)
+    for at in range(0, wide, 128):
+        block = acts_ref[:, 2 * wide + at : 2 * wide + at + 128]
+        turned = jnp.dot(block, table, preferred_element_type=f32) * scale
+        cast_ref[:, at : at + 128] = (fp_top * jnp.tanh(turned)).astype(bf16)
+    return top
+
+
+def out_mine_kernel(
+    tops_ref, acts_ref, table_ref, down_ref, part_ref, near_ref, cast_ref, top_ref
+):
+    rows = part_ref.shape[0]
+    top_ref[...] = jnp.full(top_ref.shape, cast_hidden(tops_ref, acts_ref, table_ref, cast_ref))
+    near_ref[...] = dot(cast_ref[rows:, :], down_ref[...], 1, 0).astype(bf16)
+    part_ref[...] = dot(cast_ref[:rows, :], down_ref[...], 1, 0)
+
+
+def out_their_kernel(
+    core_ref, tops_ref, acts_ref, table_ref, down_ref, part_ref,
+    keep_ref, far_ref, last_ref, cast_ref,
+):
+    rows = part_ref.shape[0]
+    cast_hidden(tops_ref, acts_ref, table_ref, cast_ref)
+    last_ref[...] = dot(cast_ref[rows:, :], down_ref[...], 1, 0).astype(bf16)
+    their = dot(cast_ref[:rows, :], down_ref[...], 1, 0)
+    place_parts(core_ref[0] == 0, part_ref[...], their, keep_ref, far_ref)
+
+
+def call(kernel, outs, scalars, arrays, limit=4 * 2**20):
+    smem, vmem = pl.BlockSpec(memory_space=pltpu.SMEM), pl.BlockSpec(memory_space=pltpu.VMEM)
+    return pl.pallas_call(
+        kernel,
+        out_shape=[jax.ShapeDtypeStruct(shape, kind) for shape, kind in outs],
+        in_specs=[smem] * len(scalars) + [vmem] * len(arrays),
+        out_specs=[vmem] * len(outs),
+        compiler_params=pltpu.CompilerParams(vmem_limit_bytes=limit),
+    )(*scalars, *arrays)
 
 
 def padded(array, dim):
@@ -280,8 +310,10 @@
         axis=0,
     )
     peaks = everyones(after(tops.max(axis=1), column))
-    gate_peak, up_peak, down_peak, token_peak = peaks[0], peaks[1], peaks[2], peaks[3]
-    pair_peak = jnp.where(jnp.arange(2 * wide) < wide, gate_peak, up_peak)[:, None]
+    in_scales = peaks[:2] / fp_top
+    small_table = after(hid_wide[:128, :128], column)
+    gate_peak, up_peak, down_peak, token_peak = (peaks[k : k + 1, None] for k in range(4))
+    pair_peak = jnp.where(jnp.arange(2 * wide)[:, None] < wide, gate_peak, up_peak)
     weight_pair = soft_cast(pair_rot, pair_peak)
     down_cast = soft_cast(down_rot, down_peak)
 
@@ -291,66 +323,59 @@
     their_tok = soft_cast(rotate_cols(their_tokens, ROT_BLOCK, rot_wide), token_peak)
     mine_tok = soft_cast(rotate_cols(mine_tokens, ROT_BLOCK, rot_wide), token_peak)
 
+    their_pair = (dot(their_tok, weight_pair, 1, 1) * 2.0**-12).astype(f16)
     mine_pair = dot(mine_tok, weight_pair, 1, 1) * 2.0**-12
-    their_pair = (dot(their_tok, weight_pair, 1, 1) * 2.0**-12).astype(f16)
-    mine_cot, their_cot = halves_along_x(after(cot_blocks, mine_pair, their_pair), first)
+    pair_blocks = sum_with_other_core(mine_pair, their_pair)
+    mine_cot, their_cot = halves_along_x(after(cot_blocks, pair_blocks, their_pair), first)
     their_back = (dot(their_cot, down_cast, 1, 1) * 2.0**-6).astype(f16)
     mine_back = dot(mine_cot, down_cast, 1, 1) * 2.0**-6
-    sums = scatter_width(
-        jnp.concatenate([mine_pair, mine_back], axis=1),
-        jnp.concatenate([their_pair, their_back], axis=1),
-        f16,
-    )
-    scales = jnp.stack(
+    back_blocks = sum_with_other_core(mine_back, their_back)
+    sums = scatter_width([pair_blocks, back_blocks], f16)
+    scales = jnp.concatenate(
         [
             token_peak * gate_peak / (fp_top * fp_top) * 2.0**12,
             token_peak * up_peak / (fp_top * fp_top) * 2.0**12,
             down_peak / fp_top * 2.0**6,
-        ]
-    )
-    vmem = pl.BlockSpec(memory_space=pltpu.VMEM)
-    acts, hidden_top = pl.pallas_call(
+        ],
+        axis=0,
+    )
+    acts, hidden_top = call(
         middle_kernel,
-        out_shape=(
-            jax.ShapeDtypeStruct(sums.shape, bf16),
-            jax.ShapeDtypeStruct((8, 128), f32),
-        ),
-        in_specs=[vmem] * 3,
-        out_specs=(vmem, vmem),
-        name="middle",
-    )(sums, jnp.broadcast_to(scales[:, None], (3, wide)), hid_wide[:128, :128])
+        [(sums.shape, bf16), ((8, 128), f32)],
+        [],
+        [sums, jnp.broadcast_to(scales, (3, wide)), small_table],
+    )
     mine_acts, their_acts = gather_half(acts)
 
     hidden_tops = copied(hidden_top.max(axis=0, keepdims=True), ALL, NY * NC * NZ * NX)
 
-    smem = pl.BlockSpec(memory_space=pltpu.SMEM)
     quarter = mine_acts.shape[0] // 2
-    in_parts = pl.pallas_call(
-        in_kernel,
-        out_shape=four_parts(quarter, features),
-        in_specs=[smem] * 2 + [vmem] * 3,
-        out_specs=[vmem] * 4,
-        name="in_part",
-    )(core[None], peaks[:2] / fp_top, mine_acts, their_acts, weight_pair)
-    in_column = sum_along_x(*in_parts)
-
-    hidden_peak = after(hidden_tops, *in_parts).max()
-    *out_parts, mine_hid_cast, their_hid_cast = pl.pallas_call(
-        out_kernel,
-        out_shape=four_parts(quarter, features)
-        + [jax.ShapeDtypeStruct((2 * quarter, wide), bf16)] * 2,
-        in_specs=[smem] * 2 + [vmem] * 4,
-        out_specs=[vmem] * 6,
-        name="out_part",
-    )(
-        core[None],
-        (HID_BLOCK**-0.5 / (hidden_peak + tiny))[None],
-        mine_acts,
-        their_acts,
-        hid_wide[:128, :128],
-        down_cast,
-    )
-    out_column = sum_along_x(*out_parts)
+    part, piece = ((quarter, features), f32), ((quarter, features), bf16)
+    in_mine, near = call(in_mine_kernel, [part, piece], [in_scales], [mine_acts, weight_pair])
+    keep, far, last = call(
+        in_their_kernel,
+        [part, piece, piece],
+        [core[None], in_scales],
+        [their_acts, weight_pair, in_mine],
+    )
+    in_column = sum_along_x(keep, far, near, last)
+
+    hidden_tops = after(hidden_tops, keep, far, last).reshape(-1, 128)
+    cast = ((2 * quarter, wide), bf16)
+    out_mine, near, mine_hid_cast, hidden_peak = call(
+        out_mine_kernel,
+        [part, piece, cast, ((8, features), f32)],
+        [],
+        [hidden_tops, mine_acts, small_table, down_cast],
+    )
+    keep, far, last, their_hid_cast = call(
+        out_their_kernel,
+        [part, piece, piece, cast],
+        [core[None]],
+        [hidden_tops, their_acts, small_table, down_cast, out_mine],
+    )
+    out_column = sum_along_x(keep, far, near, last)
+    hidden_peak = hidden_peak[:1]
 
     in_arrived = pieces_along_z(in_column)
     input_sum = in_arrived.astype(f32).sum(axis=0)
@@ -359,11 +384,11 @@
     out_sum = out_arrived.astype(f32).sum(axis=0)
     output = (out_sum * (hidden_peak * down_peak / (fp_top * fp_top))).astype(bf16)
 
-    mine_hid_cast, their_hid_cast = after((mine_hid_cast, their_hid_cast), out_parts, in_column)
+    mine_hid_cast, their_hid_cast = after((mine_hid_cast, their_hid_cast), keep)
     down_dot = dot(mine_hid_cast, mine_cot, 0, 0) + dot(their_hid_cast, their_cot, 0, 0)
-    down_grad = rotate_split(down_dot * (hidden_peak / fp_top), HID_BLOCK, hid_wide, True)
+    down_grad = rotate_split(down_dot, HID_BLOCK, hid_wide, True) * (hidden_peak / fp_top)
     down_grad = down_grad[:hid].astype(bf16)
-    mine_tok, their_tok = after((mine_tok, their_tok), out_parts, in_column)
+    mine_tok, their_tok = after((mine_tok, their_tok), keep, in_column)
     pair_dot = dot(mine_acts[:, : 2 * wide], mine_tok, 0, 0) + dot(
         their_acts[:, : 2 * wide], their_tok, 0, 0
     )

time: 212 us -> 201 us (0.948)
  waiting for transfers between devices: 59.4 us -> 72.8 us
  other arithmetic: 25 us -> 16.8 us
  matrix products: 24.2 us -> 16.4 us
  starting transfers between devices: 66.2 us -> 62.4 us
  local copies, waits for them, and re-layouts: 14.4 us -> 11.4 us
  between operations: 8.53 us -> 6.35 us
    ppermute x8, waiting for transfers between devices: 0.26 us -> 10.9 us  [along_x(): return lax.ppermute(value, ('c', 'x'), pairs)]
    dot_general x19, matrix products: 24 us -> 16.1 us  [dot(): lax.dot_general(left, right, (((left_dim,), (right_dim,)), ((), ())), pre...]
    ppermute x10, starting transfers between devices: 16.8 us -> 12.7 us  [shifted(): lax.ppermute(value, axis, [(i, (i + step) % size) for i in range(size)])]
    all_to_all x1, waiting for transfers between devices: 3.66 us -> 7.66 us  [everyones(): return lax.all_to_all(copies, ALL, 0, 0, tiled=True).max(axis=(0, 1))]
    pallas_call x4 -> x6, Pallas kernels: 13.1 us -> 11.7 us  [call(): pl.pallas_call(kernel, out_shape=[jax.ShapeDtypeStruct(shape, kind) for s...]
    unnamed x60 -> x62, local copies, waits for them, and re-layouts: 7.43 us -> 6.08 us
  transfers between devices with their start and end apart: 25 -> 26, of which waited for: 13 -> 12; matrix products, arithmetic and copies ran while one was open for 21% -> 16% of each run, Pallas kernels for 4% -> 4%
where the time goes in v2:
time: 201 us; the launch traced here: 198 us
  waiting for transfers between devices  72.8 us (36%)
  starting transfers between devices  62.4 us (31%)
  other arithmetic  16.8 us (8%)
  matrix products  16.4 us (8%)
  Pallas kernels  11.7 us (6%)
  local copies, waits for them, and re-layouts  11.4 us (6%)
  between operations  6.35 us (3%)
    ppermute x10, waiting for transfers between devices, shifted(): lax.ppermute(value, axis, [(i, (i + step) % size) for i in range(size)])  30.6 us
    all_to_all x2, starting transfers between devices, copied(): lax.all_to_all(jnp.broadcast_to(value, (count, *value.shape)), axes, 0, 0...  18.5 us
    dot_general x19, matrix products, dot(): lax.dot_general(left, right, (((left_dim,), (right_dim,)), ((), ())), pre...  16.1 us
    ppermute x10, starting transfers between devices, shifted(): lax.ppermute(value, axis, [(i, (i + step) % size) for i in range(size)])  12.7 us
    all_to_all x2, waiting for transfers between devices, pieces_along_z(): return lax.all_to_all(pieces, 'z', 0, 0, tiled=True)  12.6 us
    ppermute x8, starting transfers between devices, along_x(): return lax.ppermute(value, ('c', 'x'), pairs)  12 us
    pallas_call x6, Pallas kernels, call(): pl.pallas_call(kernel, out_shape=[jax.ShapeDtypeStruct(shape, kind) for s...  11.7 us
    all_to_all x2, starting transfers between devices, pieces_along_z(): return lax.all_to_all(pieces, 'z', 0, 0, tiled=True)  11.2 us
  transfers between devices with their start and end apart: 26, of which 12 were waited for; matrix products, arithmetic and copies ran while one was open for 16% of the time, Pallas kernels for 4%

profile of v2, /device:TPU:8, one launch (start us, length us, event | category | flops | bytes accessed | tf_op | source)
XLA Modules:
  0.0 197.8 jit_solution(17605890208982393224)
XLA Ops:
  2.4 8.5 %all-to-all-start = ((bf16[8,64,512]{2,1,0:T(8,128)(2,1)}), bf16[8,64,512]{2,1,0:T(8,128)(2,1)S(1)}, u32[]{:S(2)}, u32[]{:S(2)}) async-start(bf16[8,64,512]{2,1,0:T(8,128)(2,1)} %broadcast_in_dim.75), calls=%async_computation | async-start | bytes 1048576 | tf_op jit(solution)/shard_map/all_to_all | solution.py:98
  10.9 2.0 %fusion.28 = (bf16[512,512]{1,0:T(8,128)(2,1)S(1)}, bf16[512,512]{1,0:T(8,128)(2,1)S(1)}) fusion(s32[512]{0:T(512)S(1)} %get-tuple-element.85, s32[512]{0:T(512)S(1)} %iota.16, s32[512]{0:T(512)S(1)} %get-tuple-element.86), kind=kLoop, calls=%fused_computation.65 | loop fusion | flops 13893632 | bytes 1054720 | tf_op jit(solution)/shard_map/convert_element_type | solution.py:41
  17.8 10.6 %all-to-all-done = bf16[8,64,512]{2,1,0:T(8,128)(2,1)S(1)} async-done(((bf16[8,64,512]{2,1,0:T(8,128)(2,1)}), bf16[8,64,512]{2,1,0:T(8,128)(2,1)S(1)}, u32[]{:S(2)}, u32[]{:S(2)}) %all-to-all-start) | async-done | bytes 524320 | tf_op jit(solution)/shard_map/all_to_all | solution.py:98
  29.1 8.0 %all-to-all-start.1 = ((f32[256,1,4]{2,1,0:T(1,128)}), f32[256,1,4]{2,1,0:T(1,128)S(1)}, u32[]{:S(2)}, u32[]{:S(2)}) async-start(f32[256,1,4]{2,1,0:T(1,128)} %broadcast_in_dim.80), calls=%async_computation.1 | async-start | bytes 262144 | tf_op jit(solution)/shard_map/all_to_all | solution.py:268
  37.8 2.7 %collective-permute-start.2 = (bf16[256,512]{1,0:T(8,128)(2,1)}, bf16[256,512]{1,0:T(8,128)(2,1)S(1)}, u32[]{:S(2)}, u32[]{:S(2)}) collective-permute-start(bf16[256,512]{1,0:T(8,128)(2,1)} %bitcast.1), channel_id=1, source_target_pairs={{0,3},{1,0},{2,1},{3,2},{32,33},{33,34},{34,35},{35,32},{4,7},{5,4... | collective-permute-start | bytes 786440 | tf_op jit(solution)/shard_map/ppermute | solution.py:94
  41.3 7.7 %all-to-all-done.1 = f32[256,1,4]{2,1,0:T(1,128)S(1)} async-done(((f32[256,1,4]{2,1,0:T(1,128)}), f32[256,1,4]{2,1,0:T(1,128)S(1)}, u32[]{:S(2)}, u32[]{:S(2)}) %all-to-all-start.1) | async-done | bytes 4128 | tf_op jit(solution)/shard_map/all_to_all | solution.py:268
  51.2 2.0 %multiply_convert_fusion.2.pair_ref = bf16[1024,512]{1,0:T(8,128)(2,1)S(1)} fusion(f32[1024,512]{1,0:T(8,128)} %copy-done.9, f32[1024]{0:T(1024)S(1)} %select_add_fusion), kind=kLoop, calls=%fused_computation.19 | loop fusion | flops 1572864 | bytes 3149824 | tf_op jit(solution)/shard_map/convert_element_type | solution.py:67
  56.6 3.0 %collective-permute-start.6 = (bf16[256,512]{1,0:T(8,128)(2,1)S(1)}, bf16[256,512]{1,0:T(8,128)(2,1)S(1)}, u32[]{:S(2)}, u32[]{:S(2)}) collective-permute-start(bf16[256,512]{1,0:T(8,128)(2,1)S(1)} %bitcast.91), channel_id=1, source_target_pairs={{0,3},{1,0},{2,1},{3,2},{32,33},{33,34},{34,35},{35,32},{4,7},{5,4... | collective-permute-start | bytes 786440 | tf_op jit(solution)/shard_map/ppermute | solution.py:94
  61.9 5.9 %collective-permute-done.1 = bf16[256,512]{1,0:T(8,128)(2,1)S(1)} collective-permute-done((bf16[256,512]{1,0:T(8,128)(2,1)}, bf16[256,512]{1,0:T(8,128)(2,1)S(1)}, u32[]{:S(2)}, u32[]{:S(2)}) %collective-permute-start.1) | collective-permute-done | bytes 262176 | tf_op jit(solution)/shard_map/ppermute | solution.py:94
  68.3 2.1 %convert_add_fusion = f32[512,1024]{1,0:T(8,128)} fusion(f16[512,1024]{1,0:T(8,128)(2,1)S(1)} %collective-permute-done.3, bf16[512,512]{1,0:T(8,128)(2,1)S(1)} %fusion.10, bf16[1024,512]{1,0:T(8,128)(2,1)S(1)} %multiply_convert_fusion.2.pair_ref), kind=kOutput, calls=%fused_computation.17 | convolution fusion | flops 538443776 | bytes 4718592 | tf_op jit(solution)/shard_map/dot_general | solution.py:71
  70.4 5.0 %collective-permute-done.5 = bf16[256,512]{1,0:T(8,128)(2,1)S(1)} collective-permute-done((bf16[256,512]{1,0:T(8,128)(2,1)S(1)}, bf16[256,512]{1,0:T(8,128)(2,1)S(1)}, u32[]{:S(2)}, u32[]{:S(2)}) %collective-permute-start.5) | collective-permute-done | bytes 262176 | tf_op jit(solution)/shard_map/ppermute | solution.py:94
  76.8 1.7 fusion.73
  87.7 6.6 %collective-permute-done.9 = f16[128,1536]{1,0:T(8,128)(2,1)S(1)} collective-permute-done((f16[128,1536]{1,0:T(8,128)(2,1)S(1)}, f16[128,1536]{1,0:T(8,128)(2,1)S(1)}, u32[]{:S(2)}, u32[]{:S(2)}) %collective-permute-start.9) | collective-permute-done | bytes 393248 | tf_op jit(solution)/shard_map/ppermute | solution.py:85
  94.3 7.3 %collective-permute-done.10 = f16[128,1536]{1,0:T(8,128)(2,1)S(1)} collective-permute-done((f16[128,1536]{1,0:T(8,128)(2,1)S(1)}, f16[128,1536]{1,0:T(8,128)(2,1)S(1)}, u32[]{:S(2)}, u32[]{:S(2)}) %collective-permute-start.10) | collective-permute-done | bytes 393248 | tf_op jit(solution)/shard_map/ppermute | solution.py:85
  102.2 1.8 collective-permute-start.13
  104.7 1.9 collective-permute-start.11
  106.6 7.1 %collective-permute-done.13.got3_ref = bf16[128,1536]{1,0:T(8,128)(2,1)S(1)} collective-permute-done((bf16[128,1536]{1,0:T(8,128)(2,1)S(1)}, bf16[128,1536]{1,0:T(8,128)(2,1)S(1)}, u32[]{:S(2)}, u32[]{:S(2)}) %collective-permute-start.13) | collective-permute-done | bytes 393248 | tf_op jit(solution)/shard_map/ppermute | solution.py:85
  113.7 8.3 %collective-permute-done.12.got2_ref = bf16[128,1536]{1,0:T(8,128)(2,1)S(1)} collective-permute-done((bf16[128,1536]{1,0:T(8,128)(2,1)S(1)}, bf16[128,1536]{1,0:T(8,128)(2,1)S(1)}, u32[]{:S(2)}, u32[]{:S(2)}) %collective-permute-start.12) | collective-permute-done | bytes 393248 | tf_op jit(solution)/shard_map/ppermute | solution.py:85
  124.1 2.6 %shard_map.93.acts_ref = bf16[512,1536]{1,0:T(8,128)(2,1)} custom-call(s32[1]{0:T(128)} %bitcast.27.me_ref, bf16[128,1536]{1,0:T(8,128)(2,1)} %copy-done.4, bf16[128,1536]{1,0:T(8,128)(2,1)} %copy-done.21, bf16[128,1536]{1,0:T(8,128)(2,1)} %copy-done.20, bf16[128,1536]{1,0:T(8,128)(2,1)} %copy-done.19), custom_call_target="tpu_custom_call" | custom-call | tf_op jit(solution)/shard_map/pallas_call | solution.py:247
  127.4 10.0 %all-to-all-start.2 = ((f32[256,1,128]{2,1,0:T(1,128)}), f32[256,1,128]{2,1,0:T(1,128)S(1)}, u32[]{:S(2)}, u32[]{:S(2)}) async-start(f32[256,1,128]{2,1,0:T(1,128)} %broadcast_in_dim.87), calls=%async_computation.2 | async-start | bytes 262144 | tf_op jit(solution)/shard_map/all_to_all | solution.py:98
  139.5 1.8 shard_map.94
  141.3 2.7 %collective-permute-start.18 = (bf16[256,512]{1,0:T(8,128)(2,1)}, bf16[256,512]{1,0:T(8,128)(2,1)}, u32[]{:S(2)}, u32[]{:S(2)}) collective-permute-start(bf16[256,512]{1,0:T(8,128)(2,1)} %get-tuple-element.54), channel_id=1, source_target_pairs={{1,0},{2,1},{3,2},{0,3},{35,32},{32,33},{33,34},{34,35},{5,4},{6,5... | collective-permute-start | bytes 786440 | tf_op jit(solution)/shard_map/ppermute | solution.py:94
  144.0 2.9 %shard_map.95 = (f32[256,512]{1,0:T(8,128)S(1)}, bf16[256,512]{1,0:T(8,128)(2,1)}, bf16[256,512]{1,0:T(8,128)(2,1)}) custom-call(s32[1]{0:T(128)} %bitcast.core_ref, f32[2]{0:T(128)S(1)} %slice_multiply_fusion.1.scale_ref, bf16[512,1536]{1,0:T(8,128)(2,1)} %collective-permute-done.14.acts_ref, bf16[1024,512]{1,0:T(8,128)(2,1)S(1)} %multiply_convert_fusion.2.pair_ref, ...), custom_call_target="tpu_custom_call" | custom-call | tf_op jit(solution)/shard_map/pallas_call | solution.py:247
  150.6 2.8 %shard_map.97 = (f32[256,512]{1,0:T(8,128)S(1)}, bf16[256,512]{1,0:T(8,128)(2,1)}, bf16[256,512]{1,0:T(8,128)(2,1)}, bf16[512,512]{1,0:T(8,128)(2,1)S(1)}) custom-call(s32[1]{0:T(128)} %bitcast.core_ref, f32[256,128]{1,0:T(8,128)S(1)} %bitcast.88, bf16[512,1536]{1,0:T(8,128)(2,1)} %collective-permute-done.14.acts_ref, bf16[128,128]{1,0:T(8,128)(2,1)S(1)} %slice.57.table_ref, ...), custom_call_target="tpu_custom_call" | custom-call | tf_op jit(solution)/shard_map/pallas_call | solution.py:247
  156.4 2.5 %collective-permute-start.15 = (bf16[256,512]{1,0:T(8,128)(2,1)}, bf16[256,512]{1,0:T(8,128)(2,1)}, u32[]{:S(2)}, u32[]{:S(2)}) collective-permute-start(bf16[256,512]{1,0:T(8,128)(2,1)} %get-tuple-element.51), channel_id=1, source_target_pairs={{1,0},{2,1},{3,2},{0,3},{35,32},{32,33},{33,34},{34,35},{5,4},{6,5... | collective-permute-start | bytes 786440 | tf_op jit(solution)/shard_map/ppermute | solution.py:94
  162.1 2.0 add_convert_fusion
  164.1 7.8 %all-to-all-start.3 = ((bf16[8,32,512]{2,1,0:T(8,128)(2,1)}), bf16[8,32,512]{2,1,0:T(8,128)(2,1)S(1)}, u32[]{:S(2)}, u32[]{:S(2)}) async-start(bf16[8,32,512]{2,1,0:T(8,128)(2,1)} %bitcast.29), calls=%async_computation.3 | async-start | bytes 524288 | tf_op jit(solution)/shard_map/all_to_all | solution.py:122
  171.9 2.0 fusion.48
  176.4 2.0 add_convert_fusion.1
  179.1 4.1 %all-to-all-done.3 = bf16[8,32,512]{2,1,0:T(8,128)(2,1)S(1)} async-done(((bf16[8,32,512]{2,1,0:T(8,128)(2,1)}), bf16[8,32,512]{2,1,0:T(8,128)(2,1)S(1)}, u32[]{:S(2)}, u32[]{:S(2)}) %all-to-all-start.3) | async-done | bytes 262176 | tf_op jit(solution)/shard_map/all_to_all | solution.py:122
  183.2 3.4 %all-to-all-start.4 = ((bf16[8,32,512]{2,1,0:T(8,128)(2,1)}), bf16[8,32,512]{2,1,0:T(8,128)(2,1)S(1)}, u32[]{:S(2)}, u32[]{:S(2)}) async-start(bf16[8,32,512]{2,1,0:T(8,128)(2,1)} %bitcast.30), calls=%async_computation.4 | async-start | bytes 524288 | tf_op jit(solution)/shard_map/all_to_all | solution.py:122
  188.6 8.6 %all-to-all-done.4 = bf16[8,32,512]{2,1,0:T(8,128)(2,1)S(1)} async-done(((bf16[8,32,512]{2,1,0:T(8,128)(2,1)}), bf16[8,32,512]{2,1,0:T(8,128)(2,1)S(1)}, u32[]{:S(2)}, u32[]{:S(2)}) %all-to-all-start.4) | async-done | bytes 262176 | tf_op jit(solution)/shard_map/all_to_all | solution.py:122
  (145 shorter events, 44.5 us)
Async XLA Ops:
  0.6 12.5 %copy-start.28 = (bf16[512,448]{0,1:T(8,128)(2,1)S(1)}, bf16[512,448]{0,1:T(8,128)(2,1)}, u32[]{:S(2)}) copy-start(bf16[512,448]{0,1:T(8,128)(2,1)} %param.8) | copy-start | bytes 1376260
  0.7 12.5 %copy-start.29 = (bf16[512,448]{0,1:T(8,128)(2,1)S(1)}, bf16[512,448]{0,1:T(8,128)(2,1)}, u32[]{:S(2)}) copy-start(bf16[512,448]{0,1:T(8,128)(2,1)} %param.7) | copy-start | bytes 1376260
  2.4 26.0 %all-to-all-start = ((bf16[8,64,512]{2,1,0:T(8,128)(2,1)}), bf16[8,64,512]{2,1,0:T(8,128)(2,1)S(1)}, u32[]{:S(2)}, u32[]{:S(2)}) async-start(bf16[8,64,512]{2,1,0:T(8,128)(2,1)} %broadcast_in_dim.75), calls=%async_computation | async-start | bytes 1048576 | tf_op jit(solution)/shard_map/all_to_all | solution.py:98
  12.9 54.9 %copy-start.5 = (bf16[512,512]{1,0:T(8,128)(2,1)}, bf16[512,512]{1,0:T(8,128)(2,1)S(1)}, u32[]{:S(2)}) copy-start(bf16[512,512]{1,0:T(8,128)(2,1)S(1)} %get-tuple-element.34) | copy-start | bytes 1572868
  12.9 71.6 %copy-start.7 = (bf16[512,512]{1,0:T(8,128)(2,1)}, bf16[512,512]{1,0:T(8,128)(2,1)S(1)}, u32[]{:S(2)}) copy-start(bf16[512,512]{1,0:T(8,128)(2,1)S(1)} %get-tuple-element.35) | copy-start | bytes 1572868
  29.1 19.9 %all-to-all-start.1 = ((f32[256,1,4]{2,1,0:T(1,128)}), f32[256,1,4]{2,1,0:T(1,128)S(1)}, u32[]{:S(2)}, u32[]{:S(2)}) async-start(f32[256,1,4]{2,1,0:T(1,128)} %broadcast_in_dim.80), calls=%async_computation.1 | async-start | bytes 262144 | tf_op jit(solution)/shard_map/all_to_all | solution.py:268
  37.8 17.1 %collective-permute-start.2 = (bf16[256,512]{1,0:T(8,128)(2,1)}, bf16[256,512]{1,0:T(8,128)(2,1)S(1)}, u32[]{:S(2)}, u32[]{:S(2)}) collective-permute-start(bf16[256,512]{1,0:T(8,128)(2,1)} %bitcast.1), channel_id=1, source_target_pairs={{0,3},{1,0},{2,1},{3,2},{32,33},{33,34},{34,35},{35,32},{4,7},{5,4... | collective-permute-start | bytes 786440 | tf_op jit(solution)/shard_map/ppermute | solution.py:94
  40.5 13.4 %collective-permute-start = (bf16[256,512]{1,0:T(8,128)(2,1)}, bf16[256,512]{1,0:T(8,128)(2,1)S(1)}, u32[]{:S(2)}, u32[]{:S(2)}) collective-permute-start(bf16[256,512]{1,0:T(8,128)(2,1)} %bitcast.1), channel_id=1, source_target_pairs={{0,2},{1,3},{2,0},{3,1},{4,6},{5,7},{6,4},{7,5},{8,10},{9,11},{10,... | collective-permute-start | bytes 786440 | tf_op jit(solution)/shard_map/ppermute | solution.py:85
  56.1 12.2 %collective-permute-start.3 = (f16[512,1024]{1,0:T(8,128)(2,1)S(1)}, f16[512,1024]{1,0:T(8,128)(2,1)S(1)}, u32[]{:S(2)}, u32[]{:S(2)}) collective-permute-start(f16[512,1024]{1,0:T(8,128)(2,1)S(1)} %multiply_convert_fusion.1), channel_id=1, source_target_pairs={{0,32},{32,0},{1,33},{33,1},{2,34},{34,2},{3,35},{35,3},{4,36},{36... | collective-permute-start | bytes 3145736 | tf_op jit(solution)/shard_map/ppermute | solution.py:81
  56.2 11.6 %collective-permute-start.1 = (bf16[256,512]{1,0:T(8,128)(2,1)}, bf16[256,512]{1,0:T(8,128)(2,1)S(1)}, u32[]{:S(2)}, u32[]{:S(2)}) collective-permute-start(bf16[256,512]{1,0:T(8,128)(2,1)} %bitcast.1), channel_id=1, source_target_pairs={{0,1},{1,2},{2,3},{3,0},{32,35},{33,32},{34,33},{35,34},{4,5},{5,6... | collective-permute-start | bytes 786440 | tf_op jit(solution)/shard_map/ppermute | solution.py:94
  56.6 13.8 %collective-permute-start.6 = (bf16[256,512]{1,0:T(8,128)(2,1)S(1)}, bf16[256,512]{1,0:T(8,128)(2,1)S(1)}, u32[]{:S(2)}, u32[]{:S(2)}) collective-permute-start(bf16[256,512]{1,0:T(8,128)(2,1)S(1)} %bitcast.91), channel_id=1, source_target_pairs={{0,3},{1,0},{2,1},{3,2},{32,33},{33,34},{34,35},{35,32},{4,7},{5,4... | collective-permute-start | bytes 786440 | tf_op jit(solution)/shard_map/ppermute | solution.py:94
  59.5 15.8 %collective-permute-start.5 = (bf16[256,512]{1,0:T(8,128)(2,1)S(1)}, bf16[256,512]{1,0:T(8,128)(2,1)S(1)}, u32[]{:S(2)}, u32[]{:S(2)}) collective-permute-start(bf16[256,512]{1,0:T(8,128)(2,1)S(1)} %bitcast.92), channel_id=1, source_target_pairs={{0,1},{1,2},{2,3},{3,0},{32,35},{33,32},{34,33},{35,34},{4,5},{5,6... | collective-permute-start | bytes 786440 | tf_op jit(solution)/shard_map/ppermute | solution.py:94
  59.5 15.8 %collective-permute-start.4 = (bf16[256,512]{1,0:T(8,128)(2,1)S(1)}, bf16[256,512]{1,0:T(8,128)(2,1)S(1)}, u32[]{:S(2)}, u32[]{:S(2)}) collective-permute-start(bf16[256,512]{1,0:T(8,128)(2,1)S(1)} %bitcast.93), channel_id=1, source_target_pairs={{0,2},{1,3},{2,0},{3,1},{4,6},{5,7},{6,4},{7,5},{8,10},{9,11},{10,... | collective-permute-start | bytes 786440 | tf_op jit(solution)/shard_map/ppermute | solution.py:85
  76.7 2.3 %collective-permute-start.7 = (f16[512,512]{1,0:T(8,128)(2,1)}, f16[512,512]{1,0:T(8,128)(2,1)}, u32[]{:S(2)}, u32[]{:S(2)}) collective-permute-start(f16[512,512]{1,0:T(8,128)(2,1)} %fusion.12), channel_id=1, source_target_pairs={{0,32},{32,0},{1,33},{33,1},{2,34},{34,2},{3,35},{35,3},{4,36},{36... | collective-permute-start | bytes 1572872 | tf_op jit(solution)/shard_map/ppermute | solution.py:81
  80.7 13.6 %collective-permute-start.9 = (f16[128,1536]{1,0:T(8,128)(2,1)S(1)}, f16[128,1536]{1,0:T(8,128)(2,1)S(1)}, u32[]{:S(2)}, u32[]{:S(2)}) collective-permute-start(f16[128,1536]{1,0:T(8,128)(2,1)S(1)} %pad_maximum_fusion.3), channel_id=1, source_target_pairs={{0,128},{64,192},{128,0},{192,64},{1,129},{65,193},{129,1},{193,65... | collective-permute-start | bytes 1179656 | tf_op jit(solution)/shard_map/ppermute | solution.py:85
  82.2 19.4 %collective-permute-start.10 = (f16[128,1536]{1,0:T(8,128)(2,1)S(1)}, f16[128,1536]{1,0:T(8,128)(2,1)S(1)}, u32[]{:S(2)}, u32[]{:S(2)}) collective-permute-start(f16[128,1536]{1,0:T(8,128)(2,1)S(1)} %pad_maximum_fusion.4), channel_id=1, source_target_pairs={{0,192},{64,0},{128,64},{192,128},{1,193},{65,1},{129,65},{193,129... | collective-permute-start | bytes 1179656 | tf_op jit(solution)/shard_map/ppermute | solution.py:85
  83.6 18.0 %collective-permute-start.8 = (f16[128,1536]{1,0:T(8,128)(2,1)S(1)}, f16[128,1536]{1,0:T(8,128)(2,1)S(1)}, u32[]{:S(2)}, u32[]{:S(2)}) collective-permute-start(f16[128,1536]{1,0:T(8,128)(2,1)S(1)} %pad_maximum_fusion.2), channel_id=1, source_target_pairs={{0,64},{64,128},{128,192},{192,0},{1,65},{65,129},{129,193},{193,1... | collective-permute-start | bytes 1179656 | tf_op jit(solution)/shard_map/ppermute | solution.py:85
  102.2 21.1 %copy-start.4 = (bf16[128,1536]{1,0:T(8,128)(2,1)}, bf16[128,1536]{1,0:T(8,128)(2,1)S(1)}, u32[]{:S(2)}) copy-start(bf16[128,1536]{1,0:T(8,128)(2,1)S(1)} %get-tuple-element.43.own_ref) | copy-start | bytes 1179652
  102.2 11.4 %collective-permute-start.13 = (bf16[128,1536]{1,0:T(8,128)(2,1)S(1)}, bf16[128,1536]{1,0:T(8,128)(2,1)S(1)}, u32[]{:S(2)}, u32[]{:S(2)}) collective-permute-start(bf16[128,1536]{1,0:T(8,128)(2,1)S(1)} %get-tuple-element.43.own_ref), channel_id=1, source_target_pairs={{0,192},{64,0},{128,64},{192,128},{1,193},{65,1},{129,65},{193,129... | collective-permute-start | bytes 1179656 | tf_op jit(solution)/shard_map/ppermute | solution.py:85
  104.0 18.0 %collective-permute-start.12 = (bf16[128,1536]{1,0:T(8,128)(2,1)S(1)}, bf16[128,1536]{1,0:T(8,128)(2,1)S(1)}, u32[]{:S(2)}, u32[]{:S(2)}) collective-permute-start(bf16[128,1536]{1,0:T(8,128)(2,1)S(1)} %get-tuple-element.43.own_ref), channel_id=1, source_target_pairs={{0,128},{64,192},{128,0},{192,64},{1,129},{65,193},{129,1},{193,65... | collective-permute-start | bytes 1179656 | tf_op jit(solution)/shard_map/ppermute | solution.py:85
  104.7 18.7 %collective-permute-start.11 = (bf16[128,1536]{1,0:T(8,128)(2,1)S(1)}, bf16[128,1536]{1,0:T(8,128)(2,1)S(1)}, u32[]{:S(2)}, u32[]{:S(2)}) collective-permute-start(bf16[128,1536]{1,0:T(8,128)(2,1)S(1)} %get-tuple-element.43.own_ref), channel_id=1, source_target_pairs={{0,64},{64,128},{128,192},{192,0},{1,65},{65,129},{129,193},{193,1... | collective-permute-start | bytes 1179656 | tf_op jit(solution)/shard_map/ppermute | solution.py:85
  126.7 17.3 %collective-permute-start.14 = (bf16[512,1536]{1,0:T(8,128)(2,1)}, bf16[512,1536]{1,0:T(8,128)(2,1)}, u32[]{:S(2)}, u32[]{:S(2)}) collective-permute-start(bf16[512,1536]{1,0:T(8,128)(2,1)} %shard_map.93.acts_ref), channel_id=1, source_target_pairs={{0,32},{32,0},{1,33},{33,1},{2,34},{34,2},{3,35},{35,3},{4,36},{36... | collective-permute-start | bytes 4718600 | tf_op jit(solution)/shard_map/ppermute | solution.py:81
  127.4 22.0 %all-to-all-start.2 = ((f32[256,1,128]{2,1,0:T(1,128)}), f32[256,1,128]{2,1,0:T(1,128)S(1)}, u32[]{:S(2)}, u32[]{:S(2)}) async-start(f32[256,1,128]{2,1,0:T(1,128)} %broadcast_in_dim.87), calls=%async_computation.2 | async-start | bytes 262144 | tf_op jit(solution)/shard_map/all_to_all | solution.py:98
  141.3 19.3 %collective-permute-start.18 = (bf16[256,512]{1,0:T(8,128)(2,1)}, bf16[256,512]{1,0:T(8,128)(2,1)}, u32[]{:S(2)}, u32[]{:S(2)}) collective-permute-start(bf16[256,512]{1,0:T(8,128)(2,1)} %get-tuple-element.54), channel_id=1, source_target_pairs={{1,0},{2,1},{3,2},{0,3},{35,32},{32,33},{33,34},{34,35},{5,4},{6,5... | collective-permute-start | bytes 786440 | tf_op jit(solution)/shard_map/ppermute | solution.py:94
  147.7 14.4 %collective-permute-start.20 = (bf16[256,512]{1,0:T(8,128)(2,1)}, bf16[256,512]{1,0:T(8,128)(2,1)}, u32[]{:S(2)}, u32[]{:S(2)}) collective-permute-start(bf16[256,512]{1,0:T(8,128)(2,1)} %get-tuple-element.46), channel_id=1, source_target_pairs={{0,2},{1,3},{2,0},{3,1},{4,6},{5,7},{6,4},{7,5},{8,10},{9,11},{10,... | collective-permute-start | bytes 786440 | tf_op jit(solution)/shard_map/ppermute | solution.py:85
  148.5 13.6 %collective-permute-start.19 = (bf16[256,512]{1,0:T(8,128)(2,1)}, bf16[256,512]{1,0:T(8,128)(2,1)}, u32[]{:S(2)}, u32[]{:S(2)}) collective-permute-start(bf16[256,512]{1,0:T(8,128)(2,1)} %get-tuple-element.47), channel_id=1, source_target_pairs={{3,0},{0,1},{1,2},{2,3},{33,32},{34,33},{35,34},{32,35},{7,4},{4,5... | collective-permute-start | bytes 786440 | tf_op jit(solution)/shard_map/ppermute | solution.py:94
  156.4 20.0 %collective-permute-start.15 = (bf16[256,512]{1,0:T(8,128)(2,1)}, bf16[256,512]{1,0:T(8,128)(2,1)}, u32[]{:S(2)}, u32[]{:S(2)}) collective-permute-start(bf16[256,512]{1,0:T(8,128)(2,1)} %get-tuple-element.51), channel_id=1, source_target_pairs={{1,0},{2,1},{3,2},{0,3},{35,32},{32,33},{33,34},{34,35},{5,4},{6,5... | collective-permute-start | bytes 786440 | tf_op jit(solution)/shard_map/ppermute | solution.py:94
  158.8 17.6 %collective-permute-start.16 = (bf16[256,512]{1,0:T(8,128)(2,1)}, bf16[256,512]{1,0:T(8,128)(2,1)}, u32[]{:S(2)}, u32[]{:S(2)}) collective-permute-start(bf16[256,512]{1,0:T(8,128)(2,1)} %get-tuple-element.52), channel_id=1, source_target_pairs={{3,0},{0,1},{1,2},{2,3},{33,32},{34,33},{35,34},{32,35},{7,4},{4,5... | collective-permute-start | bytes 786440 | tf_op jit(solution)/shard_map/ppermute | solution.py:94
  159.4 12.5 %copy-start.18 = (bf16[512,512]{1,0:T(8,128)(2,1)S(1)}, bf16[512,512]{1,0:T(8,128)(2,1)}, u32[]{:S(2)}) copy-start(bf16[512,512]{1,0:T(8,128)(2,1)} %copy-done.17) | copy-start | bytes 1572868
  160.6 15.8 %collective-permute-start.17 = (bf16[256,512]{1,0:T(8,128)(2,1)}, bf16[256,512]{1,0:T(8,128)(2,1)}, u32[]{:S(2)}, u32[]{:S(2)}) collective-permute-start(bf16[256,512]{1,0:T(8,128)(2,1)} %get-tuple-element.53), channel_id=1, source_target_pairs={{0,2},{1,3},{2,0},{3,1},{4,6},{5,7},{6,4},{7,5},{8,10},{9,11},{10,... | collective-permute-start | bytes 786440 | tf_op jit(solution)/shard_map/ppermute | solution.py:85
  164.1 19.1 %all-to-all-start.3 = ((bf16[8,32,512]{2,1,0:T(8,128)(2,1)}), bf16[8,32,512]{2,1,0:T(8,128)(2,1)S(1)}, u32[]{:S(2)}, u32[]{:S(2)}) async-start(bf16[8,32,512]{2,1,0:T(8,128)(2,1)} %bitcast.29), calls=%async_computation.3 | async-start | bytes 524288 | tf_op jit(solution)/shard_map/all_to_all | solution.py:122
  183.2 13.9 %all-to-all-start.4 = ((bf16[8,32,512]{2,1,0:T(8,128)(2,1)}), bf16[8,32,512]{2,1,0:T(8,128)(2,1)S(1)}, u32[]{:S(2)}, u32[]{:S(2)}) async-start(bf16[8,32,512]{2,1,0:T(8,128)(2,1)} %bitcast.30), calls=%async_computation.4 | async-start | bytes 524288 | tf_op jit(solution)/shard_map/all_to_all | solution.py:122
  (25 other events, 97.5 us)

commit v3 on v2

--- a/solution.py
+++ b/solution.py
@@ -131,16 +131,13 @@
     me = lax.axis_index("y")
 
     def block(step):
-        picked = [
-            lax.dynamic_index_in_dim(b, (me + step) % NY, 0, keepdims=False) for b in blocks
-        ]
-        return jnp.concatenate(picked, axis=1)
+        return lax.dynamic_index_in_dim(blocks, (me + step) % NY, 0, keepdims=False)
 
     sends = [block(step).astype(kind) for step in range(1, NY)]
     total = block(0)
     for step in range(1, NY):
         total = total + shifted(sends[step - 1], "y", NY, step).astype(f32)
-    return total
+    return total, sends
 
 
 def join_kernel(me_ref, own_ref, got1_ref, got2_ref, got3_ref, out_ref):
@@ -159,14 +156,14 @@
     return mine, swapped(mine)
 
 
-def middle_kernel(sums_ref, scales_ref, table_ref, out_ref, top_ref):
+def middle_kernel(pair_ref, back_ref, scales_ref, table_ref, out_ref, top_ref):
     wide = scales_ref.shape[1]
     table = table_ref[...]
     top = jnp.zeros((8, 128), f32)
     for at in range(0, wide, 128):
-        gate = sums_ref[:, at : at + 128] * scales_ref[0:1, at : at + 128]
-        up = sums_ref[:, wide + at : wide + at + 128] * scales_ref[1:2, at : at + 128]
-        back = sums_ref[:, 2 * wide + at : 2 * wide + at + 128] * scales_ref[2:3, at : at + 128]
+        gate = pair_ref[:, at : at + 128] * scales_ref[0:1, at : at + 128]
+        up = pair_ref[:, wide + at : wide + at + 128] * scales_ref[1:2, at : at + 128]
+        back = back_ref[:, at : at + 128] * scales_ref[2:3, at : at + 128]
         sig = jax.nn.sigmoid(gate)
         hidden = (gate * sig * up).astype(bf16)
         turned = jnp.abs(jnp.dot(hidden, table, preferred_element_type=f32)) * HID_BLOCK**-0.5
@@ -326,11 +323,12 @@
     their_pair = (dot(their_tok, weight_pair, 1, 1) * 2.0**-12).astype(f16)
     mine_pair = dot(mine_tok, weight_pair, 1, 1) * 2.0**-12
     pair_blocks = sum_with_other_core(mine_pair, their_pair)
-    mine_cot, their_cot = halves_along_x(after(cot_blocks, pair_blocks, their_pair), first)
+    pair_sums, pair_sends = scatter_width(pair_blocks, f16)
+    mine_cot, their_cot = halves_along_x(after(cot_blocks, pair_sends), first)
     their_back = (dot(their_cot, down_cast, 1, 1) * 2.0**-6).astype(f16)
     mine_back = dot(mine_cot, down_cast, 1, 1) * 2.0**-6
     back_blocks = sum_with_other_core(mine_back, their_back)
-    sums = scatter_width([pair_blocks, back_blocks], f16)
+    back_sums, _ = scatter_width(back_blocks, f16)
     scales = jnp.concatenate(
         [
             token_peak * gate_peak / (fp_top * fp_top) * 2.0**12,
@@ -341,9 +339,9 @@
     )
     acts, hidden_top = call(
         middle_kernel,
-        [(sums.shape, bf16), ((8, 128), f32)],
+        [((pair_sums.shape[0], 3 * wide), bf16), ((8, 128), f32)],
         [],
-        [sums, jnp.broadcast_to(scales, (3, wide)), small_table],
+        [pair_sums, back_sums, jnp.broadcast_to(scales, (3, wide)), small_table],
     )
     mine_acts, their_acts = gather_half(acts)
 

time: 201 us -> 202 us (level)
  waiting for transfers between devices: 72.8 us -> 60 us
  starting transfers between devices: 62.4 us -> 72.6 us
    ppermute x10 -> x13, starting transfers between devices: 12.7 us -> 23.1 us  [shifted(): lax.ppermute(value, axis, [(i, (i + step) % size) for i in range(size)])]
    ppermute x10 -> x13, waiting for transfers between devices: 30.6 us -> 21.5 us  [shifted(): lax.ppermute(value, axis, [(i, (i + step) % size) for i in range(size)])]
    ppermute x8, waiting for transfers between devices: 10.9 us -> 7.58 us  [along_x(): return lax.ppermute(value, ('c', 'x'), pairs)]
    unnamed x62 -> x60, local copies, waits for them, and re-layouts: 6.08 us -> 6.09 us
  transfers between devices with their start and end apart: 26 -> 29, of which waited for: 12 -> 13; matrix products, arithmetic and copies ran while one was open for 16% -> 18% of each run, Pallas kernels for 4% -> 4%
where the time goes in v3:
time: 202 us; the launch traced here: 199 us
  starting transfers between devices  72.6 us (36%)
  waiting for transfers between devices  60 us (30%)
  other arithmetic  18.6 us (9%)
  matrix products  18.3 us (9%)
  Pallas kernels  11.7 us (6%)
  local copies, waits for them, and re-layouts  11.4 us (6%)
  between operations  5.97 us (3%)
    ppermute x13, starting transfers between devices, shifted(): lax.ppermute(value, axis, [(i, (i + step) % size) for i in range(size)])  23.1 us
    ppermute x13, waiting for transfers between devices, shifted(): lax.ppermute(value, axis, [(i, (i + step) % size) for i in range(size)])  21.5 us
    all_to_all x2, starting transfers between devices, copied(): lax.all_to_all(jnp.broadcast_to(value, (count, *value.shape)), axes, 0, 0...  18.4 us
    dot_general x19, matrix products, dot(): lax.dot_general(left, right, (((left_dim,), (right_dim,)), ((), ())), pre...  18 us
    all_to_all x2, waiting for transfers between devices, pieces_along_z(): return lax.all_to_all(pieces, 'z', 0, 0, tiled=True)  12.6 us
    ppermute x8, starting transfers between devices, along_x(): return lax.ppermute(value, ('c', 'x'), pairs)  11.9 us
    pallas_call x6, Pallas kernels, call(): pl.pallas_call(kernel, out_shape=[jax.ShapeDtypeStruct(shape, kind) for s...  11.7 us
    all_to_all x2, starting transfers between devices, pieces_along_z(): return lax.all_to_all(pieces, 'z', 0, 0, tiled=True)  11.2 us
  transfers between devices with their start and end apart: 29, of which 13 were waited for; matrix products, arithmetic and copies ran while one was open for 18% of the time, Pallas kernels for 4%

profile of v3, /device:TPU:8, one launch (start us, length us, event | category | flops | bytes accessed | tf_op | source)
XLA Modules:
  0.0 198.5 jit_solution(7469879087889270184)
XLA Ops:
  2.4 8.5 %all-to-all-start = ((bf16[8,64,512]{2,1,0:T(8,128)(2,1)}), bf16[8,64,512]{2,1,0:T(8,128)(2,1)S(1)}, u32[]{:S(2)}, u32[]{:S(2)}) async-start(bf16[8,64,512]{2,1,0:T(8,128)(2,1)} %broadcast_in_dim.75), calls=%async_computation | async-start | bytes 1048576 | tf_op jit(solution)/shard_map/all_to_all | solution.py:98
  10.9 2.0 %fusion.28 = (bf16[512,512]{1,0:T(8,128)(2,1)S(1)}, bf16[512,512]{1,0:T(8,128)(2,1)S(1)}) fusion(s32[512]{0:T(512)S(1)} %get-tuple-element.83, s32[512]{0:T(512)S(1)} %iota.16, s32[512]{0:T(512)S(1)} %get-tuple-element.84), kind=kLoop, calls=%fused_computation.65 | loop fusion | flops 13893632 | bytes 1054720 | tf_op jit(solution)/shard_map/convert_element_type | solution.py:41
  17.8 10.6 %all-to-all-done = bf16[8,64,512]{2,1,0:T(8,128)(2,1)S(1)} async-done(((bf16[8,64,512]{2,1,0:T(8,128)(2,1)}), bf16[8,64,512]{2,1,0:T(8,128)(2,1)S(1)}, u32[]{:S(2)}, u32[]{:S(2)}) %all-to-all-start) | async-done | bytes 524320 | tf_op jit(solution)/shard_map/all_to_all | solution.py:98
  29.1 8.0 %all-to-all-start.1 = ((f32[256,1,4]{2,1,0:T(1,128)}), f32[256,1,4]{2,1,0:T(1,128)S(1)}, u32[]{:S(2)}, u32[]{:S(2)}) async-start(f32[256,1,4]{2,1,0:T(1,128)} %broadcast_in_dim.80), calls=%async_computation.1 | async-start | bytes 262144 | tf_op jit(solution)/shard_map/all_to_all | solution.py:265
  37.8 2.7 %collective-permute-start.2 = (bf16[256,512]{1,0:T(8,128)(2,1)}, bf16[256,512]{1,0:T(8,128)(2,1)S(1)}, u32[]{:S(2)}, u32[]{:S(2)}) collective-permute-start(bf16[256,512]{1,0:T(8,128)(2,1)} %bitcast.1), channel_id=1, source_target_pairs={{0,3},{1,0},{2,1},{3,2},{32,33},{33,34},{34,35},{35,32},{4,7},{5,4... | collective-permute-start | bytes 786440 | tf_op jit(solution)/shard_map/ppermute | solution.py:94
  41.3 7.7 %all-to-all-done.1 = f32[256,1,4]{2,1,0:T(1,128)S(1)} async-done(((f32[256,1,4]{2,1,0:T(1,128)}), f32[256,1,4]{2,1,0:T(1,128)S(1)}, u32[]{:S(2)}, u32[]{:S(2)}) %all-to-all-start.1) | async-done | bytes 4128 | tf_op jit(solution)/shard_map/all_to_all | solution.py:265
  51.1 2.0 %multiply_convert_fusion.2.pair_ref = bf16[1024,512]{1,0:T(8,128)(2,1)S(1)} fusion(f32[1024,512]{1,0:T(8,128)} %copy-done.10, f32[1024]{0:T(1024)S(1)} %select_add_fusion), kind=kLoop, calls=%fused_computation.19 | loop fusion | flops 1572864 | bytes 3149824 | tf_op jit(solution)/shard_map/convert_element_type | solution.py:67
  57.9 3.0 %collective-permute-start.9 = (bf16[256,512]{1,0:T(8,128)(2,1)S(1)}, bf16[256,512]{1,0:T(8,128)(2,1)S(1)}, u32[]{:S(2)}, u32[]{:S(2)}) collective-permute-start(bf16[256,512]{1,0:T(8,128)(2,1)S(1)} %bitcast.101), channel_id=1, source_target_pairs={{0,3},{1,0},{2,1},{3,2},{32,33},{33,34},{34,35},{35,32},{4,7},{5,4... | collective-permute-start | bytes 786440 | tf_op jit(solution)/shard_map/ppermute | solution.py:94
  64.4 4.3 %collective-permute-done.1 = bf16[256,512]{1,0:T(8,128)(2,1)S(1)} collective-permute-done((bf16[256,512]{1,0:T(8,128)(2,1)}, bf16[256,512]{1,0:T(8,128)(2,1)S(1)}, u32[]{:S(2)}, u32[]{:S(2)}) %collective-permute-start.1) | collective-permute-done | bytes 262176 | tf_op jit(solution)/shard_map/ppermute | solution.py:94
  70.2 2.2 %convert_add_fusion = f32[512,1024]{1,0:T(8,128)S(1)} fusion(f16[512,1024]{1,0:T(8,128)(2,1)} %collective-permute-done.3, bf16[512,512]{1,0:T(8,128)(2,1)S(1)} %fusion.10, bf16[1024,512]{1,0:T(8,128)(2,1)S(1)} %multiply_convert_fusion.2.pair_ref), kind=kOutput, calls=%fused_computation.17 | convolution fusion | flops 538443776 | bytes 4718592 | tf_op jit(solution)/shard_map/dot_general | solution.py:71
  73.4 3.3 %collective-permute-done.8 = bf16[256,512]{1,0:T(8,128)(2,1)S(1)} collective-permute-done((bf16[256,512]{1,0:T(8,128)(2,1)S(1)}, bf16[256,512]{1,0:T(8,128)(2,1)S(1)}, u32[]{:S(2)}, u32[]{:S(2)}) %collective-permute-start.8) | collective-permute-done | bytes 262176 | tf_op jit(solution)/shard_map/ppermute | solution.py:94
  86.1 2.7 %collective-permute-start.11 = (f16[128,512]{1,0:T(8,128)(2,1)S(1)}, f16[128,512]{1,0:T(8,128)(2,1)S(1)}, u32[]{:S(2)}, u32[]{:S(2)}) collective-permute-start(f16[128,512]{1,0:T(8,128)(2,1)S(1)} %get-tuple-element.70), channel_id=1, source_target_pairs={{0,64},{64,128},{128,192},{192,0},{1,65},{65,129},{129,193},{193,1... | collective-permute-start | bytes 393224 | tf_op jit(solution)/shard_map/ppermute | solution.py:85
  90.5 6.6 %collective-permute-start.12 = (f16[128,512]{1,0:T(8,128)(2,1)S(1)}, f16[128,512]{1,0:T(8,128)(2,1)S(1)}, u32[]{:S(2)}, u32[]{:S(2)}) collective-permute-start(f16[128,512]{1,0:T(8,128)(2,1)S(1)} %get-tuple-element.72), channel_id=1, source_target_pairs={{0,128},{64,192},{128,0},{192,64},{1,129},{65,193},{129,1},{193,65... | collective-permute-start | bytes 393224 | tf_op jit(solution)/shard_map/ppermute | solution.py:85
  99.2 3.5 %collective-permute-done.12 = f16[128,512]{1,0:T(8,128)(2,1)S(1)} collective-permute-done((f16[128,512]{1,0:T(8,128)(2,1)S(1)}, f16[128,512]{1,0:T(8,128)(2,1)S(1)}, u32[]{:S(2)}, u32[]{:S(2)}) %collective-permute-start.12) | collective-permute-done | bytes 131104 | tf_op jit(solution)/shard_map/ppermute | solution.py:85
  103.2 2.5 %collective-permute-start.16 = (bf16[128,1536]{1,0:T(8,128)(2,1)S(1)}, bf16[128,1536]{1,0:T(8,128)(2,1)S(1)}, u32[]{:S(2)}, u32[]{:S(2)}) collective-permute-start(bf16[128,1536]{1,0:T(8,128)(2,1)S(1)} %get-tuple-element.43.own_ref), channel_id=1, source_target_pairs={{0,192},{64,0},{128,64},{192,128},{1,193},{65,1},{129,65},{193,129... | collective-permute-start | bytes 1179656 | tf_op jit(solution)/shard_map/ppermute | solution.py:85
  106.3 2.5 %collective-permute-start.14 = (bf16[128,1536]{1,0:T(8,128)(2,1)S(1)}, bf16[128,1536]{1,0:T(8,128)(2,1)S(1)}, u32[]{:S(2)}, u32[]{:S(2)}) collective-permute-start(bf16[128,1536]{1,0:T(8,128)(2,1)S(1)} %get-tuple-element.43.own_ref), channel_id=1, source_target_pairs={{0,64},{64,128},{128,192},{192,0},{1,65},{65,129},{129,193},{193,1... | collective-permute-start | bytes 1179656 | tf_op jit(solution)/shard_map/ppermute | solution.py:85
  108.8 6.4 %collective-permute-done.16.got3_ref = bf16[128,1536]{1,0:T(8,128)(2,1)S(1)} collective-permute-done((bf16[128,1536]{1,0:T(8,128)(2,1)S(1)}, bf16[128,1536]{1,0:T(8,128)(2,1)S(1)}, u32[]{:S(2)}, u32[]{:S(2)}) %collective-permute-start.16) | collective-permute-done | bytes 393248 | tf_op jit(solution)/shard_map/ppermute | solution.py:85
  115.3 8.0 %collective-permute-done.15.got2_ref = bf16[128,1536]{1,0:T(8,128)(2,1)S(1)} collective-permute-done((bf16[128,1536]{1,0:T(8,128)(2,1)S(1)}, bf16[128,1536]{1,0:T(8,128)(2,1)S(1)}, u32[]{:S(2)}, u32[]{:S(2)}) %collective-permute-start.15) | collective-permute-done | bytes 393248 | tf_op jit(solution)/shard_map/ppermute | solution.py:85
  124.9 2.6 %shard_map.93.acts_ref = bf16[512,1536]{1,0:T(8,128)(2,1)} custom-call(s32[1]{0:T(128)} %bitcast.27.me_ref, bf16[128,1536]{1,0:T(8,128)(2,1)} %copy-done.4, bf16[128,1536]{1,0:T(8,128)(2,1)} %copy-done.21, bf16[128,1536]{1,0:T(8,128)(2,1)} %copy-done.20, bf16[128,1536]{1,0:T(8,128)(2,1)} %copy-done.19), custom_call_target="tpu_custom_call" | custom-call | tf_op jit(solution)/shard_map/pallas_call | solution.py:244
  128.3 9.9 %all-to-all-start.2 = ((f32[256,1,128]{2,1,0:T(1,128)}), f32[256,1,128]{2,1,0:T(1,128)S(1)}, u32[]{:S(2)}, u32[]{:S(2)}) async-start(f32[256,1,128]{2,1,0:T(1,128)} %broadcast_in_dim.87), calls=%async_computation.2 | async-start | bytes 262144 | tf_op jit(solution)/shard_map/all_to_all | solution.py:98
  140.2 1.8 shard_map.94
  142.1 2.7 %collective-permute-start.21 = (bf16[256,512]{1,0:T(8,128)(2,1)}, bf16[256,512]{1,0:T(8,128)(2,1)}, u32[]{:S(2)}, u32[]{:S(2)}) collective-permute-start(bf16[256,512]{1,0:T(8,128)(2,1)} %get-tuple-element.54), channel_id=1, source_target_pairs={{1,0},{2,1},{3,2},{0,3},{35,32},{32,33},{33,34},{34,35},{5,4},{6,5... | collective-permute-start | bytes 786440 | tf_op jit(solution)/shard_map/ppermute | solution.py:94
  144.7 2.9 %shard_map.95 = (f32[256,512]{1,0:T(8,128)S(1)}, bf16[256,512]{1,0:T(8,128)(2,1)}, bf16[256,512]{1,0:T(8,128)(2,1)}) custom-call(s32[1]{0:T(128)} %bitcast.core_ref, f32[2]{0:T(128)S(1)} %slice_multiply_fusion.1.scale_ref, bf16[512,1536]{1,0:T(8,128)(2,1)} %collective-permute-done.17.acts_ref, bf16[1024,512]{1,0:T(8,128)(2,1)S(1)} %multiply_convert_fusion.2.pair_ref, ...), custom_call_target="tpu_custom_call" | custom-call | tf_op jit(solution)/shard_map/pallas_call | solution.py:244
  151.4 2.8 %shard_map.97 = (f32[256,512]{1,0:T(8,128)S(1)}, bf16[256,512]{1,0:T(8,128)(2,1)}, bf16[256,512]{1,0:T(8,128)(2,1)}, bf16[512,512]{1,0:T(8,128)(2,1)S(1)}) custom-call(s32[1]{0:T(128)} %bitcast.core_ref, f32[256,128]{1,0:T(8,128)S(1)} %bitcast.96, bf16[512,1536]{1,0:T(8,128)(2,1)} %collective-permute-done.17.acts_ref, bf16[128,128]{1,0:T(8,128)(2,1)S(1)} %slice.57.table_ref, ...), custom_call_target="tpu_custom_call" | custom-call | tf_op jit(solution)/shard_map/pallas_call | solution.py:244
  157.1 2.5 %collective-permute-start.18 = (bf16[256,512]{1,0:T(8,128)(2,1)}, bf16[256,512]{1,0:T(8,128)(2,1)}, u32[]{:S(2)}, u32[]{:S(2)}) collective-permute-start(bf16[256,512]{1,0:T(8,128)(2,1)} %get-tuple-element.51), channel_id=1, source_target_pairs={{1,0},{2,1},{3,2},{0,3},{35,32},{32,33},{33,34},{34,35},{5,4},{6,5... | collective-permute-start | bytes 786440 | tf_op jit(solution)/shard_map/ppermute | solution.py:94
  162.9 2.0 add_convert_fusion
  164.9 7.8 %all-to-all-start.3 = ((bf16[8,32,512]{2,1,0:T(8,128)(2,1)}), bf16[8,32,512]{2,1,0:T(8,128)(2,1)S(1)}, u32[]{:S(2)}, u32[]{:S(2)}) async-start(bf16[8,32,512]{2,1,0:T(8,128)(2,1)} %bitcast.29), calls=%async_computation.3 | async-start | bytes 524288 | tf_op jit(solution)/shard_map/all_to_all | solution.py:122
  172.7 2.0 fusion.48
  177.2 1.9 add_convert_fusion.1
  179.9 4.1 %all-to-all-done.3 = bf16[8,32,512]{2,1,0:T(8,128)(2,1)S(1)} async-done(((bf16[8,32,512]{2,1,0:T(8,128)(2,1)}), bf16[8,32,512]{2,1,0:T(8,128)(2,1)S(1)}, u32[]{:S(2)}, u32[]{:S(2)}) %all-to-all-start.3) | async-done | bytes 262176 | tf_op jit(solution)/shard_map/all_to_all | solution.py:122
  184.0 3.4 %all-to-all-start.4 = ((bf16[8,32,512]{2,1,0:T(8,128)(2,1)}), bf16[8,32,512]{2,1,0:T(8,128)(2,1)S(1)}, u32[]{:S(2)}, u32[]{:S(2)}) async-start(bf16[8,32,512]{2,1,0:T(8,128)(2,1)} %bitcast.30), calls=%async_computation.4 | async-start | bytes 524288 | tf_op jit(solution)/shard_map/all_to_all | solution.py:122
  189.3 8.5 %all-to-all-done.4 = bf16[8,32,512]{2,1,0:T(8,128)(2,1)S(1)} async-done(((bf16[8,32,512]{2,1,0:T(8,128)(2,1)}), bf16[8,32,512]{2,1,0:T(8,128)(2,1)S(1)}, u32[]{:S(2)}, u32[]{:S(2)}) %all-to-all-start.4) | async-done | bytes 262176 | tf_op jit(solution)/shard_map/all_to_all | solution.py:122
  (147 shorter events, 51.3 us)
Async XLA Ops:
  2.4 26.0 %all-to-all-start = ((bf16[8,64,512]{2,1,0:T(8,128)(2,1)}), bf16[8,64,512]{2,1,0:T(8,128)(2,1)S(1)}, u32[]{:S(2)}, u32[]{:S(2)}) async-start(bf16[8,64,512]{2,1,0:T(8,128)(2,1)} %broadcast_in_dim.75), calls=%async_computation | async-start | bytes 1048576 | tf_op jit(solution)/shard_map/all_to_all | solution.py:98
  12.9 55.8 %copy-start.5 = (bf16[512,512]{1,0:T(8,128)(2,1)}, bf16[512,512]{1,0:T(8,128)(2,1)S(1)}, u32[]{:S(2)}) copy-start(bf16[512,512]{1,0:T(8,128)(2,1)S(1)} %get-tuple-element.34) | copy-start | bytes 1572868
  12.9 65.1 %copy-start.7 = (bf16[512,512]{1,0:T(8,128)(2,1)}, bf16[512,512]{1,0:T(8,128)(2,1)S(1)}, u32[]{:S(2)}) copy-start(bf16[512,512]{1,0:T(8,128)(2,1)S(1)} %get-tuple-element.35) | copy-start | bytes 1572868
  29.1 19.9 %all-to-all-start.1 = ((f32[256,1,4]{2,1,0:T(1,128)}), f32[256,1,4]{2,1,0:T(1,128)S(1)}, u32[]{:S(2)}, u32[]{:S(2)}) async-start(f32[256,1,4]{2,1,0:T(1,128)} %broadcast_in_dim.80), calls=%async_computation.1 | async-start | bytes 262144 | tf_op jit(solution)/shard_map/all_to_all | solution.py:265
  37.8 17.6 %collective-permute-start.2 = (bf16[256,512]{1,0:T(8,128)(2,1)}, bf16[256,512]{1,0:T(8,128)(2,1)S(1)}, u32[]{:S(2)}, u32[]{:S(2)}) collective-permute-start(bf16[256,512]{1,0:T(8,128)(2,1)} %bitcast.1), channel_id=1, source_target_pairs={{0,3},{1,0},{2,1},{3,2},{32,33},{33,34},{34,35},{35,32},{4,7},{5,4... | collective-permute-start | bytes 786440 | tf_op jit(solution)/shard_map/ppermute | solution.py:94
  40.5 13.2 %collective-permute-start = (bf16[256,512]{1,0:T(8,128)(2,1)}, bf16[256,512]{1,0:T(8,128)(2,1)S(1)}, u32[]{:S(2)}, u32[]{:S(2)}) collective-permute-start(bf16[256,512]{1,0:T(8,128)(2,1)} %bitcast.1), channel_id=1, source_target_pairs={{0,2},{1,3},{2,0},{3,1},{4,6},{5,7},{6,4},{7,5},{8,10},{9,11},{10,... | collective-permute-start | bytes 786440 | tf_op jit(solution)/shard_map/ppermute | solution.py:85
  57.6 12.6 %collective-permute-start.3 = (f16[512,1024]{1,0:T(8,128)(2,1)}, f16[512,1024]{1,0:T(8,128)(2,1)}, u32[]{:S(2)}, u32[]{:S(2)}) collective-permute-start(f16[512,1024]{1,0:T(8,128)(2,1)} %multiply_convert_fusion.1), channel_id=1, source_target_pairs={{0,32},{32,0},{1,33},{33,1},{2,34},{34,2},{3,35},{35,3},{4,36},{36... | collective-permute-start | bytes 3145736 | tf_op jit(solution)/shard_map/ppermute | solution.py:81
  57.6 11.1 %collective-permute-start.1 = (bf16[256,512]{1,0:T(8,128)(2,1)}, bf16[256,512]{1,0:T(8,128)(2,1)S(1)}, u32[]{:S(2)}, u32[]{:S(2)}) collective-permute-start(bf16[256,512]{1,0:T(8,128)(2,1)} %bitcast.1), channel_id=1, source_target_pairs={{0,1},{1,2},{2,3},{3,0},{32,35},{33,32},{34,33},{35,34},{4,5},{5,6... | collective-permute-start | bytes 786440 | tf_op jit(solution)/shard_map/ppermute | solution.py:94
  57.9 15.5 %collective-permute-start.9 = (bf16[256,512]{1,0:T(8,128)(2,1)S(1)}, bf16[256,512]{1,0:T(8,128)(2,1)S(1)}, u32[]{:S(2)}, u32[]{:S(2)}) collective-permute-start(bf16[256,512]{1,0:T(8,128)(2,1)S(1)} %bitcast.101), channel_id=1, source_target_pairs={{0,3},{1,0},{2,1},{3,2},{32,33},{33,34},{34,35},{35,32},{4,7},{5,4... | collective-permute-start | bytes 786440 | tf_op jit(solution)/shard_map/ppermute | solution.py:94
  60.8 15.8 %collective-permute-start.8 = (bf16[256,512]{1,0:T(8,128)(2,1)S(1)}, bf16[256,512]{1,0:T(8,128)(2,1)S(1)}, u32[]{:S(2)}, u32[]{:S(2)}) collective-permute-start(bf16[256,512]{1,0:T(8,128)(2,1)S(1)} %bitcast.102), channel_id=1, source_target_pairs={{0,1},{1,2},{2,3},{3,0},{32,35},{33,32},{34,33},{35,34},{4,5},{5,6... | collective-permute-start | bytes 786440 | tf_op jit(solution)/shard_map/ppermute | solution.py:94
  60.8 15.8 %collective-permute-start.7 = (bf16[256,512]{1,0:T(8,128)(2,1)S(1)}, bf16[256,512]{1,0:T(8,128)(2,1)S(1)}, u32[]{:S(2)}, u32[]{:S(2)}) collective-permute-start(bf16[256,512]{1,0:T(8,128)(2,1)S(1)} %bitcast.103), channel_id=1, source_target_pairs={{0,2},{1,3},{2,0},{3,1},{4,6},{5,7},{6,4},{7,5},{8,10},{9,11},{10,... | collective-permute-start | bytes 786440 | tf_op jit(solution)/shard_map/ppermute | solution.py:85
  78.0 6.6 %collective-permute-start.10 = (f16[512,512]{1,0:T(8,128)(2,1)}, f16[512,512]{1,0:T(8,128)(2,1)S(1)}, u32[]{:S(2)}, u32[]{:S(2)}) collective-permute-start(f16[512,512]{1,0:T(8,128)(2,1)} %fusion.12), channel_id=1, source_target_pairs={{0,32},{32,0},{1,33},{33,1},{2,34},{34,2},{3,35},{35,3},{4,36},{36... | collective-permute-start | bytes 1572872 | tf_op jit(solution)/shard_map/ppermute | solution.py:81
  81.1 9.4 %collective-permute-start.4 = (f16[128,1024]{1,0:T(8,128)(2,1)}, f16[128,1024]{1,0:T(8,128)(2,1)S(1)}, u32[]{:S(2)}, u32[]{:S(2)}) collective-permute-start(f16[128,1024]{1,0:T(8,128)(2,1)} %get-tuple-element.65), channel_id=1, source_target_pairs={{0,64},{64,128},{128,192},{192,0},{1,65},{65,129},{129,193},{193,1... | collective-permute-start | bytes 786440 | tf_op jit(solution)/shard_map/ppermute | solution.py:85
  81.6 15.4 %collective-permute-start.6 = (f16[128,1024]{1,0:T(8,128)(2,1)}, f16[128,1024]{1,0:T(8,128)(2,1)S(1)}, u32[]{:S(2)}, u32[]{:S(2)}) collective-permute-start(f16[128,1024]{1,0:T(8,128)(2,1)} %get-tuple-element.66), channel_id=1, source_target_pairs={{0,192},{64,0},{128,64},{192,128},{1,193},{65,1},{129,65},{193,129... | collective-permute-start | bytes 786440 | tf_op jit(solution)/shard_map/ppermute | solution.py:85
  83.1 14.5 %collective-permute-start.5 = (f16[128,1024]{1,0:T(8,128)(2,1)}, f16[128,1024]{1,0:T(8,128)(2,1)S(1)}, u32[]{:S(2)}, u32[]{:S(2)}) collective-permute-start(f16[128,1024]{1,0:T(8,128)(2,1)} %get-tuple-element.67), channel_id=1, source_target_pairs={{0,128},{64,192},{128,0},{192,64},{1,129},{65,193},{129,1},{193,65... | collective-permute-start | bytes 786440 | tf_op jit(solution)/shard_map/ppermute | solution.py:85
  86.1 12.7 %collective-permute-start.11 = (f16[128,512]{1,0:T(8,128)(2,1)S(1)}, f16[128,512]{1,0:T(8,128)(2,1)S(1)}, u32[]{:S(2)}, u32[]{:S(2)}) collective-permute-start(f16[128,512]{1,0:T(8,128)(2,1)S(1)} %get-tuple-element.70), channel_id=1, source_target_pairs={{0,64},{64,128},{128,192},{192,0},{1,65},{65,129},{129,193},{193,1... | collective-permute-start | bytes 393224 | tf_op jit(solution)/shard_map/ppermute | solution.py:85
  88.8 10.4 %collective-permute-start.13 = (f16[128,512]{1,0:T(8,128)(2,1)S(1)}, f16[128,512]{1,0:T(8,128)(2,1)S(1)}, u32[]{:S(2)}, u32[]{:S(2)}) collective-permute-start(f16[128,512]{1,0:T(8,128)(2,1)S(1)} %get-tuple-element.71), channel_id=1, source_target_pairs={{0,192},{64,0},{128,64},{192,128},{1,193},{65,1},{129,65},{193,129... | collective-permute-start | bytes 393224 | tf_op jit(solution)/shard_map/ppermute | solution.py:85
  90.5 12.2 %collective-permute-start.12 = (f16[128,512]{1,0:T(8,128)(2,1)S(1)}, f16[128,512]{1,0:T(8,128)(2,1)S(1)}, u32[]{:S(2)}, u32[]{:S(2)}) collective-permute-start(f16[128,512]{1,0:T(8,128)(2,1)S(1)} %get-tuple-element.72), channel_id=1, source_target_pairs={{0,128},{64,192},{128,0},{192,64},{1,129},{65,193},{129,1},{193,65... | collective-permute-start | bytes 393224 | tf_op jit(solution)/shard_map/ppermute | solution.py:85
  103.2 21.0 %copy-start.4 = (bf16[128,1536]{1,0:T(8,128)(2,1)}, bf16[128,1536]{1,0:T(8,128)(2,1)S(1)}, u32[]{:S(2)}) copy-start(bf16[128,1536]{1,0:T(8,128)(2,1)S(1)} %get-tuple-element.43.own_ref) | copy-start | bytes 1179652
  103.2 12.0 %collective-permute-start.16 = (bf16[128,1536]{1,0:T(8,128)(2,1)S(1)}, bf16[128,1536]{1,0:T(8,128)(2,1)S(1)}, u32[]{:S(2)}, u32[]{:S(2)}) collective-permute-start(bf16[128,1536]{1,0:T(8,128)(2,1)S(1)} %get-tuple-element.43.own_ref), channel_id=1, source_target_pairs={{0,192},{64,0},{128,64},{192,128},{1,193},{65,1},{129,65},{193,129... | collective-permute-start | bytes 1179656 | tf_op jit(solution)/shard_map/ppermute | solution.py:85
  105.8 17.5 %collective-permute-start.15 = (bf16[128,1536]{1,0:T(8,128)(2,1)S(1)}, bf16[128,1536]{1,0:T(8,128)(2,1)S(1)}, u32[]{:S(2)}, u32[]{:S(2)}) collective-permute-start(bf16[128,1536]{1,0:T(8,128)(2,1)S(1)} %get-tuple-element.43.own_ref), channel_id=1, source_target_pairs={{0,128},{64,192},{128,0},{192,64},{1,129},{65,193},{129,1},{193,65... | collective-permute-start | bytes 1179656 | tf_op jit(solution)/shard_map/ppermute | solution.py:85
  106.3 17.9 %collective-permute-start.14 = (bf16[128,1536]{1,0:T(8,128)(2,1)S(1)}, bf16[128,1536]{1,0:T(8,128)(2,1)S(1)}, u32[]{:S(2)}, u32[]{:S(2)}) collective-permute-start(bf16[128,1536]{1,0:T(8,128)(2,1)S(1)} %get-tuple-element.43.own_ref), channel_id=1, source_target_pairs={{0,64},{64,128},{128,192},{192,0},{1,65},{65,129},{129,193},{193,1... | collective-permute-start | bytes 1179656 | tf_op jit(solution)/shard_map/ppermute | solution.py:85
  127.5 17.2 %collective-permute-start.17 = (bf16[512,1536]{1,0:T(8,128)(2,1)}, bf16[512,1536]{1,0:T(8,128)(2,1)}, u32[]{:S(2)}, u32[]{:S(2)}) collective-permute-start(bf16[512,1536]{1,0:T(8,128)(2,1)} %shard_map.93.acts_ref), channel_id=1, source_target_pairs={{0,32},{32,0},{1,33},{33,1},{2,34},{34,2},{3,35},{35,3},{4,36},{36... | collective-permute-start | bytes 4718600 | tf_op jit(solution)/shard_map/ppermute | solution.py:81
  128.3 21.9 %all-to-all-start.2 = ((f32[256,1,128]{2,1,0:T(1,128)}), f32[256,1,128]{2,1,0:T(1,128)S(1)}, u32[]{:S(2)}, u32[]{:S(2)}) async-start(f32[256,1,128]{2,1,0:T(1,128)} %broadcast_in_dim.87), calls=%async_computation.2 | async-start | bytes 262144 | tf_op jit(solution)/shard_map/all_to_all | solution.py:98
  142.1 19.3 %collective-permute-start.21 = (bf16[256,512]{1,0:T(8,128)(2,1)}, bf16[256,512]{1,0:T(8,128)(2,1)}, u32[]{:S(2)}, u32[]{:S(2)}) collective-permute-start(bf16[256,512]{1,0:T(8,128)(2,1)} %get-tuple-element.54), channel_id=1, source_target_pairs={{1,0},{2,1},{3,2},{0,3},{35,32},{32,33},{33,34},{34,35},{5,4},{6,5... | collective-permute-start | bytes 786440 | tf_op jit(solution)/shard_map/ppermute | solution.py:94
  148.4 14.5 %collective-permute-start.23 = (bf16[256,512]{1,0:T(8,128)(2,1)}, bf16[256,512]{1,0:T(8,128)(2,1)}, u32[]{:S(2)}, u32[]{:S(2)}) collective-permute-start(bf16[256,512]{1,0:T(8,128)(2,1)} %get-tuple-element.46), channel_id=1, source_target_pairs={{0,2},{1,3},{2,0},{3,1},{4,6},{5,7},{6,4},{7,5},{8,10},{9,11},{10,... | collective-permute-start | bytes 786440 | tf_op jit(solution)/shard_map/ppermute | solution.py:85
  149.3 13.6 %collective-permute-start.22 = (bf16[256,512]{1,0:T(8,128)(2,1)}, bf16[256,512]{1,0:T(8,128)(2,1)}, u32[]{:S(2)}, u32[]{:S(2)}) collective-permute-start(bf16[256,512]{1,0:T(8,128)(2,1)} %get-tuple-element.47), channel_id=1, source_target_pairs={{3,0},{0,1},{1,2},{2,3},{33,32},{34,33},{35,34},{32,35},{7,4},{4,5... | collective-permute-start | bytes 786440 | tf_op jit(solution)/shard_map/ppermute | solution.py:94
  157.1 20.1 %collective-permute-start.18 = (bf16[256,512]{1,0:T(8,128)(2,1)}, bf16[256,512]{1,0:T(8,128)(2,1)}, u32[]{:S(2)}, u32[]{:S(2)}) collective-permute-start(bf16[256,512]{1,0:T(8,128)(2,1)} %get-tuple-element.51), channel_id=1, source_target_pairs={{1,0},{2,1},{3,2},{0,3},{35,32},{32,33},{33,34},{34,35},{5,4},{6,5... | collective-permute-start | bytes 786440 | tf_op jit(solution)/shard_map/ppermute | solution.py:94
  159.6 17.6 %collective-permute-start.19 = (bf16[256,512]{1,0:T(8,128)(2,1)}, bf16[256,512]{1,0:T(8,128)(2,1)}, u32[]{:S(2)}, u32[]{:S(2)}) collective-permute-start(bf16[256,512]{1,0:T(8,128)(2,1)} %get-tuple-element.52), channel_id=1, source_target_pairs={{3,0},{0,1},{1,2},{2,3},{33,32},{34,33},{35,34},{32,35},{7,4},{4,5... | collective-permute-start | bytes 786440 | tf_op jit(solution)/shard_map/ppermute | solution.py:94
  161.3 15.8 %collective-permute-start.20 = (bf16[256,512]{1,0:T(8,128)(2,1)}, bf16[256,512]{1,0:T(8,128)(2,1)}, u32[]{:S(2)}, u32[]{:S(2)}) collective-permute-start(bf16[256,512]{1,0:T(8,128)(2,1)} %get-tuple-element.53), channel_id=1, source_target_pairs={{0,2},{1,3},{2,0},{3,1},{4,6},{5,7},{6,4},{7,5},{8,10},{9,11},{10,... | collective-permute-start | bytes 786440 | tf_op jit(solution)/shard_map/ppermute | solution.py:85
  164.9 19.1 %all-to-all-start.3 = ((bf16[8,32,512]{2,1,0:T(8,128)(2,1)}), bf16[8,32,512]{2,1,0:T(8,128)(2,1)S(1)}, u32[]{:S(2)}, u32[]{:S(2)}) async-start(bf16[8,32,512]{2,1,0:T(8,128)(2,1)} %bitcast.29), calls=%async_computation.3 | async-start | bytes 524288 | tf_op jit(solution)/shard_map/all_to_all | solution.py:122
  184.0 13.9 %all-to-all-start.4 = ((bf16[8,32,512]{2,1,0:T(8,128)(2,1)}), bf16[8,32,512]{2,1,0:T(8,128)(2,1)S(1)}, u32[]{:S(2)}, u32[]{:S(2)}) async-start(bf16[8,32,512]{2,1,0:T(8,128)(2,1)} %bitcast.30), calls=%async_computation.4 | async-start | bytes 524288 | tf_op jit(solution)/shard_map/all_to_all | solution.py:122
  (27 other events, 145.1 us)
